TPU v7x, 128 devices: a whole 4x4x4 slice. The times are simulated.
128 devices in a mesh: dp: 8 (over x, z_hi), tp: 16 (over z_lo, y, core).
Axes of the slice: x: 4, y: 4, z: 4 (z_hi: 2, z_lo: 2; z = z_hi * 2 + z_lo), core: 2. Of those that a mesh axis runs over, the one named last changes fastest.
Arguments:
- hidden_in: bfloat16 [4, 64, 4096], P(None, 'dp'), may hold values from -6 to 6
- pre_gain: float32 [4096], replicated, may hold values from 0.25 to 1.75
- w_zx: bfloat16 [4096, 2, 8192], P(None, None, 'tp'), may hold values from -0.09375 to 0.09375
- zx_codes: bfloat16 [4096, 2, 8192], P(('dp', 'tp')), may hold values from -4 to 4
- zx_exponents: int32 [32, 2, 64], P('dp', None, 'tp'), may hold values from -9 to -6
- w_bc: bfloat16 [4096, 2048], P(None, 'tp'), may hold values from -0.09375 to 0.09375
- w_dt: bfloat16 [4096, 128], P(None, 'tp'), may hold values from -0.09375 to 0.09375
- conv_x: float32 [5, 8192], P(None, 'tp'), may hold values from -0.6 to 0.6
- conv_bc: float32 [5, 2048], P(None, 'tp'), may hold values from -0.6 to 0.6
- dt_bias: float32 [128], P('tp'), may hold values from -2 to 0.5
- decay_rate: float32 [128], P('tp'), may hold values from 0.05 to 2
- skip_gain: float32 [128], P('tp'), may hold values from 0.5 to 1.5
- conv_state_x: bfloat16 [64, 3, 8192], P('dp', None, 'tp'), may hold values from -6 to 6
- conv_state_bc: bfloat16 [64, 3, 2048], P('dp', None, 'tp'), may hold values from -6 to 6
- ssm_state: float32 [64, 128, 64, 256], P('dp', 'tp'), may hold values from -6 to 6
- norm_gain: float32 [8192], P('tp'), may hold values from 0.25 to 1.75
- w_out: bfloat16 [8192, 4096], P('tp'), may hold values from -0.0625 to 0.0625
- out_codes: bfloat16 [8192, 4096], P('tp', 'dp'), may hold values from -4 to 4
- out_exponents: int32 [64, 32], P('tp', 'dp'), may hold values from -7 to -4
Outputs:
- mixed: bfloat16 [4, 64, 4096], P(None, 'dp', 'tp')
- final_state: float32 [64, 128, 64, 256], P('dp', 'tp')
All inputs are finite; a program needn't handle non-finite values.
Results may differ from a plain program's by a relative error of at most 0.014.
Values may be sent and summed in bfloat16 or wider, within the bound.
No kernel may reach another device: no remote copies, remote signals or barrier semaphores. Data moves between devices by JAX's collectives and lax.ppermute only.
A program may use at most 128 MiB of HBM per device.

v0:
```python
import jax
import jax.numpy as jnp
from jax import lax
from jax.sharding import PartitionSpec as P

H = 128
G = 4
BLK = 128
STEPS = 4
DI = 8192


EPS = 1e-05


def joined_along(tiles, dim):
    lengths = list(tiles.shape[1:])
    lengths[dim] *= tiles.shape[0]
    return jnp.moveaxis(tiles, 0, dim).reshape(lengths)


def copy_for_each(value, axis):
    devices = lax.axis_size(axis)
    return lax.all_to_all(
        jnp.broadcast_to(value[None], (devices, *value.shape)), axis, 0, 0, tiled=True
    )


def gather_directly(value, axis, dim):
    return joined_along(copy_for_each(value, axis), dim)


def cut_along(value, dim, devices):
    before, after = (value.shape[:dim], value.shape[dim + 1 :])
    return jnp.moveaxis(value.reshape(*before, devices, -1, *after), dim, 0)


def sent_and_summed(value, axis, dim):
    devices = lax.axis_size(axis)
    tiles = lax.all_to_all(cut_along(value, dim, devices), axis, 0, 0, tiled=True)
    return jnp.sum(tiles, axis=0)


def of_everyone(value, axis):
    return copy_for_each(value, axis).sum(axis=0)


def decode_pairs(codes, exponents, block):
    rows, pair, cols = codes.shape
    blocked = codes.astype(jnp.float32).reshape(rows // block, block, pair, cols // block, block)
    scales = jnp.exp2(exponents.astype(jnp.float32))
    return (blocked * scales[:, None, :, :, None]).reshape(rows, pair, cols)


def decode_matrix(codes, exponents, block):
    rows, cols = codes.shape
    blocked = codes.astype(jnp.float32).reshape(rows // block, block, cols // block, block)
    scales = jnp.exp2(exponents.astype(jnp.float32))
    return (blocked * scales[:, None, :, None]).reshape(rows, cols)


def conv_step(history, fresh, params):
    window = jnp.concatenate([history, fresh[:, None, :]], axis=1)
    mixed = jnp.sum(window * params[:4][None], axis=1) + params[4]
    return (jax.nn.silu(mixed), window[:, 1:])


def body(
    hidden_in,
    pre_gain,
    w_zx,
    zx_codes,
    zx_exponents,
    w_bc,
    w_dt,
    conv_x,
    conv_bc,
    dt_bias,
    decay_rate,
    skip_gain,
    conv_state_x,
    conv_state_bc,
    ssm_state,
    norm_gain,
    w_out,
    out_codes,
    out_exponents,
):
    replica = lax.axis_index("dp")
    slot = lax.axis_index("tp")
    traded = lax.all_to_all(zx_codes, "tp", split_axis=2, concat_axis=0, tiled=True)
    zx_delta = decode_pairs(traded, zx_exponents, BLK)
    row_span = traded.shape[0]
    local_cols = traded.shape[2]
    w_rows = lax.dynamic_slice_in_dim(w_zx, replica * row_span, row_span, 0)
    zx_weights = (
        (w_rows.astype(jnp.float32) + zx_delta)
        .astype(jnp.bfloat16)
        .reshape(row_span, 2 * local_cols)
    )
    out_piece = decode_matrix(out_codes, out_exponents, BLK).astype(jnp.bfloat16)
    out_full = lax.all_gather(out_piece, "dp", axis=1, tiled=True)
    new_out = (w_out.astype(jnp.float32) + out_full.astype(jnp.float32)).astype(jnp.bfloat16)
    heads_here = ssm_state.shape[1]
    states_n = ssm_state.shape[3]
    group = slot * heads_here // (H // G)
    group_mask = (jnp.arange(G) == group).astype(jnp.float32)
    history_x = conv_state_x.astype(jnp.float32)
    history_bc = conv_state_bc.astype(jnp.float32)
    state = ssm_state
    results = []
    carried = None
    for step in range(STEPS):
        x = hidden_in[step].astype(jnp.float32)
        if step > 0:
            x = x + carried.astype(jnp.float32)
        rows = x.shape[0]
        normed = (x * lax.rsqrt(jnp.mean(x * x, -1, keepdims=True) + EPS) * pre_gain).astype(
            jnp.bfloat16
        )
        everyone = gather_directly(normed, "dp", 0)
        own_cols = lax.dynamic_slice_in_dim(everyone, replica * row_span, row_span, 1)
        zx = sent_and_summed(
            jnp.dot(own_cols, zx_weights, preferred_element_type=jnp.float32), "dp", 0
        )
        zx = zx.reshape(rows, 2, local_cols)
        gate = zx[:, 0]
        inner = zx[:, 1]
        bc_raw = jnp.dot(normed, w_bc, preferred_element_type=jnp.float32)
        dt_raw = jnp.dot(normed, w_dt, preferred_element_type=jnp.float32)
        conv_inner, history_x = conv_step(history_x, inner, conv_x)
        conv_piece, history_bc = conv_step(history_bc, bc_raw, conv_bc)
        bc_all = gather_directly(conv_piece, "tp", 1)
        b_group = lax.dynamic_slice_in_dim(bc_all, group * states_n, states_n, 1)
        c_group = lax.dynamic_slice_in_dim(bc_all, G * states_n + group * states_n, states_n, 1)
        step_size = jax.nn.softplus(dt_raw + dt_bias)
        decay = jnp.exp(-step_size * decay_rate)
        inner_heads = conv_inner.reshape(rows, heads_here, -1)
        state = (
            decay[:, :, None, None] * state
            + (step_size[:, :, None] * inner_heads)[:, :, :, None] * b_group[:, None, None, :]
        )
        read = (
            jnp.einsum("rhpn,rn->rhp", state, c_group, precision=lax.Precision.HIGHEST)
            + skip_gain[:, None] * inner_heads
        )
        gated = read.reshape(rows, local_cols) * jax.nn.silu(gate)
        squares = jnp.sum(gated * gated, -1)
        totals = of_everyone(squares[:, None] * group_mask, "tp")
        mean_sq = jnp.sum(totals * group_mask, -1) / (DI // G)
        scaled = (gated * lax.rsqrt(mean_sq + EPS)[:, None] * norm_gain).astype(jnp.bfloat16)
        partial_value = jnp.dot(scaled, new_out, preferred_element_type=jnp.float32)
        summed = sent_and_summed(partial_value, "tp", 1).astype(jnp.bfloat16)
        results.append(summed)
        if step + 1 < STEPS:
            carried = gather_directly(summed, "tp", 1)
    return (jnp.stack(results), state)


def solution(mesh):
    return jax.shard_map(
        body,
        mesh=mesh,
        in_specs=(
            P(None, "dp", None),
            P(),
            P(None, None, "tp"),
            P(("dp", "tp"), None, None),
            P("dp", None, "tp"),
            P(None, "tp"),
            P(None, "tp"),
            P(None, "tp"),
            P(None, "tp"),
            P("tp"),
            P("tp"),
            P("tp"),
            P("dp", None, "tp"),
            P("dp", None, "tp"),
            P("dp", "tp", None, None),
            P("tp"),
            P("tp", None),
            P("tp", "dp"),
            P("tp", "dp"),
        ),
        out_specs=(P(None, "dp", "tp"), P("dp", "tp", None, None)),
        check_vma=False,
    )
```

profile of v0, /device:TPU:1, one launch (start us, length us, event | category | flops | bytes accessed | tf_op | source)
XLA Modules:
  0.0 413.4 jit_solution(10557720529095760822)
XLA Ops:
  10.4 7.4 %copy.32 = bf16[32,2,8192]{0,1,2:T(2,128)(2,1)} copy(bf16[32,2,8192]{2,1,0:T(2,128)(2,1)S(1)} %copy-done.4) | data formatting | bytes 2097152 | tf_op args[3]
  17.8 10.0 %reshape.669 = bf16[16,2,16384]{2,1,0:T(2,128)(2,1)} reshape(bf16[8192,2,32]{2,1,0:T(2,128)(2,1)} %bitcast.196) | data formatting | bytes 2097152
  27.8 7.3 %all-to-all-start.1 = ((bf16[16,2,16384]{2,1,0:T(2,128)(2,1)}), bf16[16,2,16384]{2,1,0:T(2,128)(2,1)S(1)}, u32[]{:S(2)}, u32[]{:S(2)}) async-start(bf16[16,2,16384]{2,1,0:T(2,128)(2,1)} %reshape.669), calls=%async_computation.1 | async-start | bytes 2097152 | tf_op jit(solution)/shard_map/all_to_all | solution.py:91
  42.1 8.8 %all-to-all-done.1 = bf16[16,2,16384]{2,1,0:T(2,128)(2,1)S(1)} async-done(((bf16[16,2,16384]{2,1,0:T(2,128)(2,1)}), bf16[16,2,16384]{2,1,0:T(2,128)(2,1)S(1)}, u32[]{:S(2)}, u32[]{:S(2)}) %all-to-all-start.1) | async-done | bytes 1048608 | tf_op jit(solution)/shard_map/all_to_all | solution.py:91
  51.7 7.0 %all-to-all-start = ((bf16[8,8,4096]{2,1,0:T(8,128)(2,1)}), bf16[8,8,4096]{2,1,0:T(8,128)(2,1)}, u32[]{:S(2)}, u32[]{:S(2)}) async-start(bf16[8,8,4096]{2,1,0:T(8,128)(2,1)} %broadcast_in_dim.47), calls=%async_computation | async-start | bytes 1048576 | tf_op jit(solution)/shard_map/all_to_all | solution.py:24
  62.2 8.9 %convert_bitcast_fusion = f32[16,32,2,512]{1,2,3,0:T(2,128)} fusion(bf16[32,2,16,512]{0,1,3,2:T(2,128)(2,1)} %bitcast.195), kind=kLoop, calls=%fused_computation | loop fusion | flops 524288 | bytes 3145728 | tf_op jit(solution)/shard_map/convert_element_type | solution.py:50
  71.1 11.6 %copy.33 = f32[16,32,2,512]{3,2,1,0:T(2,128)} copy(f32[16,32,2,512]{1,2,3,0:T(2,128)} %convert_bitcast_fusion) | data formatting | bytes 4194304 | tf_op jit(solution)/shard_map/convert_element_type | solution.py:50
  98.4 6.9 %all-to-all-start.2 = ((f32[8,8,1024]{2,1,0:T(8,128)}), f32[8,8,1024]{2,1,0:T(8,128)S(1)}, u32[]{:S(2)}, u32[]{:S(2)}) async-start(f32[8,8,1024]{2,1,0:T(8,128)} %fusion.49), calls=%async_computation.2 | async-start | bytes 524288 | tf_op jit(solution)/shard_map/all_to_all | solution.py:40
  106.9 5.9 %all-to-all-done.2 = f32[8,8,1024]{2,1,0:T(8,128)S(1)} async-done(((f32[8,8,1024]{2,1,0:T(8,128)}), f32[8,8,1024]{2,1,0:T(8,128)S(1)}, u32[]{:S(2)}, u32[]{:S(2)}) %all-to-all-start.2) | async-done | bytes 262176 | tf_op jit(solution)/shard_map/all_to_all | solution.py:40
  113.7 7.6 %fusion.1 = f32[8,1,8,64]{3,1,2,0:T(1,128)S(1)} fusion(f32[8,8,64,256]{3,2,1,0:T(8,128)} %param.33, f32[8,256]{1,0:T(8,128)S(1)} %get-tuple-element.17, f32[8,8,64]{2,1,0:T(8,128)S(1)} %broadcast_multiply_fusion.3, f32[8,8]{1,0:T(8,128)S(1)} %get-tuple-element.26, f32[8,256,1,1]{1,0,2,3:T(8,128)S(1)} %get-tuple-element.16), kind=kOutput, calls=%fused_computation.7 | convolution fusion | flops 15728640 | bytes 4243712 | tf_op jit(solution)/shard_map/rhpn,rn->rhp/dot_general | solution.py:144
  127.6 5.8 %all-to-all-done.4 = f32[16,8,4]{1,2,0:T(4,128)S(1)} async-done(((f32[16,8,4]{1,2,0:T(4,128)}), f32[16,8,4]{1,2,0:T(4,128)S(1)}, u32[]{:S(2)}, u32[]{:S(2)}) %all-to-all-start.4) | async-done | bytes 2080 | tf_op jit(solution)/shard_map/all_to_all | solution.py:24
  133.7 7.3 %fusion = bf16[4096,512]{0,1:T(8,128)(2,1)} fusion(bf16[512,4096]{1,0:T(8,128)(2,1)} %all-gather.2.cloned.1.call-done, bf16[512,4096]{1,0:T(8,128)(2,1)} %param.35), kind=kLoop, calls=%fused_computation.2 | loop fusion | flops 8388608 | bytes 12582912 | tf_op jit(solution)/shard_map/dot_general | solution.py:152
  141.0 6.5 %copy.46 = bf16[4096,512]{1,0:T(8,128)(2,1)} copy(bf16[4096,512]{0,1:T(8,128)(2,1)} %fusion) | data formatting | bytes 8388608 | tf_op jit(solution)/shard_map/dot_general | solution.py:152
  155.3 6.1 %all-to-all-done.5 = f32[16,8,256]{2,1,0:T(8,128)S(1)} async-done(((f32[16,8,256]{2,1,0:T(8,128)}), f32[16,8,256]{2,1,0:T(8,128)S(1)}, u32[]{:S(2)}, u32[]{:S(2)}) %all-to-all-start.5) | async-done | bytes 131104 | tf_op jit(solution)/shard_map/all_to_all | solution.py:40
  166.0 5.9 %all-to-all-done.6 = bf16[16,8,256]{2,1,0:T(8,128)(2,1)S(1)} async-done(((bf16[16,8,256]{2,1,0:T(8,128)(2,1)}), bf16[16,8,256]{2,1,0:T(8,128)(2,1)S(1)}, u32[]{:S(2)}, u32[]{:S(2)}) %all-to-all-start.6) | async-done | bytes 65568 | tf_op jit(solution)/shard_map/all_to_all | solution.py:24
  176.8 10.2 %all-to-all-done.7 = bf16[8,8,4096]{2,1,0:T(8,128)(2,1)S(1)} async-done(((bf16[8,8,4096]{2,1,0:T(8,128)(2,1)}), bf16[8,8,4096]{2,1,0:T(8,128)(2,1)S(1)}, u32[]{:S(2)}, u32[]{:S(2)}) %all-to-all-start.7) | async-done | bytes 524320 | tf_op jit(solution)/shard_map/all_to_all | solution.py:24
  201.6 7.2 %all-to-all-done.8 = f32[8,8,1024]{2,1,0:T(8,128)S(1)} async-done(((f32[8,8,1024]{2,1,0:T(8,128)}), f32[8,8,1024]{2,1,0:T(8,128)S(1)}, u32[]{:S(2)}, u32[]{:S(2)}) %all-to-all-start.8) | async-done | bytes 262176 | tf_op jit(solution)/shard_map/all_to_all | solution.py:40
  209.1 7.6 %fusion.11 = f32[8,1,8,64]{3,1,2,0:T(1,128)S(1)} fusion(f32[8,8,64,256]{3,2,1,0:T(8,128)} %param.33, f32[8,256]{1,0:T(8,128)S(1)} %get-tuple-element.15, f32[8,8,64]{2,1,0:T(8,128)S(1)} %broadcast_multiply_fusion.2, f32[8,8]{1,0:T(8,128)S(1)} %get-tuple-element.28, f32[8,256]{1,0:T(8,128)S(1)} %get-tuple-element.17, ...), kind=kOutput, calls=%fused_computation.22 | convolution fusion | flops 18874368 | bytes 4268544 | tf_op jit(solution)/shard_map/rhpn,rn->rhp/dot_general | solution.py:144
  217.0 10.2 %all_to_all.124 = f32[16,8,4]{1,2,0:T(4,128)S(1)} all-to-all(f32[16,8,4]{1,2,0:T(4,128)S(1)} %broadcast_in_dim.56), channel_id=1, replica_groups=mesh['dp'=8,'tp'=16] {'tp'}, dimensions={0} | all-to-all | bytes 4096 | tf_op jit(solution)/shard_map/all_to_all | solution.py:24
  235.3 6.1 %all-to-all-done.11 = f32[16,8,256]{2,1,0:T(8,128)S(1)} async-done(((f32[16,8,256]{2,1,0:T(8,128)}), f32[16,8,256]{2,1,0:T(8,128)S(1)}, u32[]{:S(2)}, u32[]{:S(2)}) %all-to-all-start.11) | async-done | bytes 131104 | tf_op jit(solution)/shard_map/all_to_all | solution.py:40
  245.9 5.9 %all-to-all-done.12 = bf16[16,8,256]{2,1,0:T(8,128)(2,1)S(1)} async-done(((bf16[16,8,256]{2,1,0:T(8,128)(2,1)}), bf16[16,8,256]{2,1,0:T(8,128)(2,1)S(1)}, u32[]{:S(2)}, u32[]{:S(2)}) %all-to-all-start.12) | async-done | bytes 65568 | tf_op jit(solution)/shard_map/all_to_all | solution.py:24
  256.7 10.4 %all-to-all-done.13 = bf16[8,8,4096]{2,1,0:T(8,128)(2,1)S(1)} async-done(((bf16[8,8,4096]{2,1,0:T(8,128)(2,1)}), bf16[8,8,4096]{2,1,0:T(8,128)(2,1)S(1)}, u32[]{:S(2)}, u32[]{:S(2)}) %all-to-all-start.13) | async-done | bytes 524320 | tf_op jit(solution)/shard_map/all_to_all | solution.py:24
  281.7 7.4 %all-to-all-done.14 = f32[8,8,1024]{2,1,0:T(8,128)S(1)} async-done(((f32[8,8,1024]{2,1,0:T(8,128)}), f32[8,8,1024]{2,1,0:T(8,128)S(1)}, u32[]{:S(2)}, u32[]{:S(2)}) %all-to-all-start.14) | async-done | bytes 262176 | tf_op jit(solution)/shard_map/all_to_all | solution.py:40
  289.3 8.0 %fusion.2 = f32[8,1,8,64]{3,1,2,0:T(1,128)S(1)} fusion(f32[8,256]{1,0:T(8,128)S(1)} %get-tuple-element.13, f32[8,8,64]{2,1,0:T(8,128)S(1)} %broadcast_multiply_fusion.1, f32[8,8]{1,0:T(8,128)S(1)} %get-tuple-element.30, f32[8,8,64,256]{3,2,1,0:T(8,128)} %param.33, f32[8,256]{1,0:T(8,128)S(1)} %get-tuple-element.15, ...), kind=kOutput, calls=%fused_computation.8 | convolution fusion | flops 22020096 | bytes 4293376 | tf_op jit(solution)/shard_map/rhpn,rn->rhp/dot_general | solution.py:144
  297.6 10.0 %all_to_all.125 = f32[16,8,4]{1,2,0:T(4,128)S(1)} all-to-all(f32[16,8,4]{1,2,0:T(4,128)S(1)} %broadcast_in_dim.62), channel_id=1, replica_groups=mesh['dp'=8,'tp'=16] {'tp'}, dimensions={0} | all-to-all | bytes 4096 | tf_op jit(solution)/shard_map/all_to_all | solution.py:24
  315.7 6.1 %all-to-all-done.17 = f32[16,8,256]{2,1,0:T(8,128)S(1)} async-done(((f32[16,8,256]{2,1,0:T(8,128)}), f32[16,8,256]{2,1,0:T(8,128)S(1)}, u32[]{:S(2)}, u32[]{:S(2)}) %all-to-all-start.17) | async-done | bytes 131104 | tf_op jit(solution)/shard_map/all_to_all | solution.py:40
  326.3 5.9 %all-to-all-done.18 = bf16[16,8,256]{2,1,0:T(8,128)(2,1)S(1)} async-done(((bf16[16,8,256]{2,1,0:T(8,128)(2,1)}), bf16[16,8,256]{2,1,0:T(8,128)(2,1)S(1)}, u32[]{:S(2)}, u32[]{:S(2)}) %all-to-all-start.18) | async-done | bytes 65568 | tf_op jit(solution)/shard_map/all_to_all | solution.py:24
  337.2 10.4 %all-to-all-done.19 = bf16[8,8,4096]{2,1,0:T(8,128)(2,1)S(1)} async-done(((bf16[8,8,4096]{2,1,0:T(8,128)(2,1)}), bf16[8,8,4096]{2,1,0:T(8,128)(2,1)S(1)}, u32[]{:S(2)}, u32[]{:S(2)}) %all-to-all-start.19) | async-done | bytes 524320 | tf_op jit(solution)/shard_map/all_to_all | solution.py:24
  362.1 7.4 %all-to-all-done.20 = f32[8,8,1024]{2,1,0:T(8,128)S(1)} async-done(((f32[8,8,1024]{2,1,0:T(8,128)}), f32[8,8,1024]{2,1,0:T(8,128)S(1)}, u32[]{:S(2)}, u32[]{:S(2)}) %all-to-all-start.20) | async-done | bytes 262176 | tf_op jit(solution)/shard_map/all_to_all | solution.py:40
  369.8 6.2 %multiply_add_fusion = f32[8,8,64,256]{3,2,1,0:T(8,128)S(1)} fusion(f32[8,256]{1,0:T(8,128)S(1)} %get-tuple-element.11, f32[8,8,64]{2,1,0:T(8,128)S(1)} %broadcast_multiply_fusion, f32[8,8]{1,0:T(8,128)S(1)} %get-tuple-element.32, f32[8,256]{1,0:T(8,128)S(1)} %get-tuple-element.13, f32[8,8,64]{2,1,0:T(8,128)S(1)} %broadcast_multiply_fusion.1, ...), kind=kLoop, calls=%fused_computation.3 | loop fusion | flops 12582912 | bytes 8487936 | tf_op jit(solution)/shard_map/add | solution.py:140
  383.3 10.0 %all_to_all.126 = f32[16,8,4]{1,2,0:T(4,128)S(1)} all-to-all(f32[16,8,4]{1,2,0:T(4,128)S(1)} %broadcast_in_dim.68), channel_id=1, replica_groups=mesh['dp'=8,'tp'=16] {'tp'}, dimensions={0} | all-to-all | bytes 4096 | tf_op jit(solution)/shard_map/all_to_all | solution.py:24
  397.0 8.9 %all_to_all.127 = f32[16,8,256]{2,1,0:T(8,128)S(1)} all-to-all(f32[16,8,256]{2,1,0:T(8,128)S(1)} %convolution_bitcast_fusion), channel_id=1, replica_groups=mesh['dp'=8,'tp'=16] {'tp'}, dimensions={0} | all-to-all | bytes 262144 | tf_op jit(solution)/shard_map/all_to_all | solution.py:40
  (198 shorter events, 147.8 us)
Async XLA Ops:
  7.2 28.2 %copy-start = (bf16[4096,128]{1,0:T(8,128)(2,1)S(1)}, bf16[4096,128]{1,0:T(8,128)(2,1)}, u32[]{:S(2)}) copy-start(bf16[4096,128]{1,0:T(8,128)(2,1)} %param.24) | copy-start | bytes 3145732
  7.2 126.6 %all-gather.2.cloned.1.call-start = ((), (), s32[]{:S(2)}) async-start(), calls=%async_computation.24 | async-start | bytes 4718592 | tf_op jit(solution)/shard_map/all_gather | solution.py:102
  17.8 17.4 %copy-start.2 = (bf16[4,8,4096]{2,1,0:T(8,128)(2,1)S(1)}, bf16[4,8,4096]{2,1,0:T(8,128)(2,1)}, u32[]{:S(2)}) copy-start(bf16[4,8,4096]{2,1,0:T(8,128)(2,1)} %param.19) | copy-start | bytes 786436
  17.8 17.6 %copy-start.3 = (f32[4096]{0:T(1024)S(1)}, f32[4096]{0:T(1024)}, u32[]{:S(2)}) copy-start(f32[4096]{0:T(1024)} %param.20) | copy-start | bytes 49156
  17.8 17.9 %copy-start.5 = (bf16[4096,8]{0,1:T(8,128)(2,1)S(1)}, bf16[4096,8]{0,1:T(8,128)(2,1)}, u32[]{:S(2)}) copy-start(bf16[4096,8]{0,1:T(8,128)(2,1)} %param.25) | copy-start | bytes 196612
  17.8 17.9 %copy-start.9 = (f32[8]{0:T(128)S(1)}, f32[8]{0:T(128)}, u32[]{:S(2)}) copy-start(f32[8]{0:T(128)} %param.29) | copy-start | bytes 100
  17.8 17.9 %copy-start.10 = (f32[8]{0:T(128)S(1)}, f32[8]{0:T(128)}, u32[]{:S(2)}) copy-start(f32[8]{0:T(128)} %param.28) | copy-start | bytes 100
  17.8 18.7 %copy-start.12 = (s32[4,2,4]{2,1,0:T(2,128)S(1)}, s32[4,2,4]{2,1,0:T(2,128)}, u32[]{:S(2)}) copy-start(s32[4,2,4]{2,1,0:T(2,128)} %param.23) | copy-start | bytes 388
  27.8 23.1 %all-to-all-start.1 = ((bf16[16,2,16384]{2,1,0:T(2,128)(2,1)}), bf16[16,2,16384]{2,1,0:T(2,128)(2,1)S(1)}, u32[]{:S(2)}, u32[]{:S(2)}) async-start(bf16[16,2,16384]{2,1,0:T(2,128)(2,1)} %reshape.669), calls=%async_computation.1 | async-start | bytes 2097152 | tf_op jit(solution)/shard_map/all_to_all | solution.py:91
  51.7 35.9 %all-to-all-start = ((bf16[8,8,4096]{2,1,0:T(8,128)(2,1)}), bf16[8,8,4096]{2,1,0:T(8,128)(2,1)}, u32[]{:S(2)}, u32[]{:S(2)}) async-start(bf16[8,8,4096]{2,1,0:T(8,128)(2,1)} %broadcast_in_dim.47), calls=%async_computation | async-start | bytes 1048576 | tf_op jit(solution)/shard_map/all_to_all | solution.py:24
  82.8 24.0 %copy-start.6 = (bf16[8,3,512]{2,0,1:T(8,128)(2,1)S(1)}, bf16[8,3,512]{2,0,1:T(8,128)(2,1)}, u32[]{:S(2)}) copy-start(bf16[8,3,512]{2,0,1:T(8,128)(2,1)} %param.31) | copy-start | bytes 73732
  86.8 34.5 %copy-start.7 = (f32[8]{0:T(128)S(1)}, f32[8]{0:T(128)}, u32[]{:S(2)}) copy-start(f32[8]{0:T(128)} %param.30) | copy-start | bytes 100
  87.6 40.0 %copy-start.13 = (f32[512]{0:T(512)S(1)}, f32[512]{0:T(512)}, u32[]{:S(2)}) copy-start(f32[512]{0:T(512)} %param.34) | copy-start | bytes 6148
  88.2 10.2 %all-to-all-start.3 = ((f32[16,8,128]{2,1,0:T(8,128)}), f32[16,8,128]{2,1,0:T(8,128)S(1)}, u32[]{:S(2)}, u32[]{:S(2)}) async-start(f32[16,8,128]{2,1,0:T(8,128)} %broadcast_in_dim.49), calls=%async_computation.3 | async-start | bytes 131072 | tf_op jit(solution)/shard_map/all_to_all | solution.py:24
  98.4 14.3 %all-to-all-start.2 = ((f32[8,8,1024]{2,1,0:T(8,128)}), f32[8,8,1024]{2,1,0:T(8,128)S(1)}, u32[]{:S(2)}, u32[]{:S(2)}) async-start(f32[8,8,1024]{2,1,0:T(8,128)} %fusion.49), calls=%async_computation.2 | async-start | bytes 524288 | tf_op jit(solution)/shard_map/all_to_all | solution.py:40
  122.3 11.2 %all-to-all-start.4 = ((f32[16,8,4]{1,2,0:T(4,128)}), f32[16,8,4]{1,2,0:T(4,128)S(1)}, u32[]{:S(2)}, u32[]{:S(2)}) async-start(f32[16,8,4]{1,2,0:T(4,128)} %broadcast_in_dim.50), calls=%async_computation.4 | async-start | bytes 65536 | tf_op jit(solution)/shard_map/all_to_all | solution.py:24
  151.5 49.9 %copy-start.11 = (f32[8]{0:T(128)S(1)}, f32[8]{0:T(128)}, u32[]{:S(2)}) copy-start(f32[8]{0:T(128)} %param.28) | copy-start | bytes 100
  151.5 10.0 %all-to-all-start.5 = ((f32[16,8,256]{2,1,0:T(8,128)}), f32[16,8,256]{2,1,0:T(8,128)S(1)}, u32[]{:S(2)}, u32[]{:S(2)}) async-start(f32[16,8,256]{2,1,0:T(8,128)} %convolution_bitcast_fusion.3), calls=%async_computation.5 | async-start | bytes 262144 | tf_op jit(solution)/shard_map/all_to_all | solution.py:40
  162.1 9.7 %all-to-all-start.6 = ((bf16[16,8,256]{2,1,0:T(8,128)(2,1)}), bf16[16,8,256]{2,1,0:T(8,128)(2,1)S(1)}, u32[]{:S(2)}, u32[]{:S(2)}) async-start(bf16[16,8,256]{2,1,0:T(8,128)(2,1)} %broadcast_in_dim.51), calls=%async_computation.6 | async-start | bytes 131072 | tf_op jit(solution)/shard_map/all_to_all | solution.py:24
  173.0 14.0 %all-to-all-start.7 = ((bf16[8,8,4096]{2,1,0:T(8,128)(2,1)}), bf16[8,8,4096]{2,1,0:T(8,128)(2,1)S(1)}, u32[]{:S(2)}, u32[]{:S(2)}) async-start(bf16[8,8,4096]{2,1,0:T(8,128)(2,1)} %broadcast_in_dim.53), calls=%async_computation.7 | async-start | bytes 1048576 | tf_op jit(solution)/shard_map/all_to_all | solution.py:24
  187.7 10.3 %all-to-all-start.9 = ((f32[16,8,128]{2,1,0:T(8,128)}), f32[16,8,128]{2,1,0:T(8,128)S(1)}, u32[]{:S(2)}, u32[]{:S(2)}) async-start(f32[16,8,128]{2,1,0:T(8,128)} %broadcast_in_dim.55), calls=%async_computation.9 | async-start | bytes 131072 | tf_op jit(solution)/shard_map/all_to_all | solution.py:24
  198.0 10.8 %all-to-all-start.8 = ((f32[8,8,1024]{2,1,0:T(8,128)}), f32[8,8,1024]{2,1,0:T(8,128)S(1)}, u32[]{:S(2)}, u32[]{:S(2)}) async-start(f32[8,8,1024]{2,1,0:T(8,128)} %fusion.47), calls=%async_computation.8 | async-start | bytes 524288 | tf_op jit(solution)/shard_map/all_to_all | solution.py:40
  231.6 9.8 %all-to-all-start.11 = ((f32[16,8,256]{2,1,0:T(8,128)}), f32[16,8,256]{2,1,0:T(8,128)S(1)}, u32[]{:S(2)}, u32[]{:S(2)}) async-start(f32[16,8,256]{2,1,0:T(8,128)} %convolution_bitcast_fusion.2), calls=%async_computation.11 | async-start | bytes 262144 | tf_op jit(solution)/shard_map/all_to_all | solution.py:40
  242.0 9.7 %all-to-all-start.12 = ((bf16[16,8,256]{2,1,0:T(8,128)(2,1)}), bf16[16,8,256]{2,1,0:T(8,128)(2,1)S(1)}, u32[]{:S(2)}, u32[]{:S(2)}) async-start(bf16[16,8,256]{2,1,0:T(8,128)(2,1)} %broadcast_in_dim.57), calls=%async_computation.12 | async-start | bytes 131072 | tf_op jit(solution)/shard_map/all_to_all | solution.py:24
  253.0 14.2 %all-to-all-start.13 = ((bf16[8,8,4096]{2,1,0:T(8,128)(2,1)}), bf16[8,8,4096]{2,1,0:T(8,128)(2,1)S(1)}, u32[]{:S(2)}, u32[]{:S(2)}) async-start(bf16[8,8,4096]{2,1,0:T(8,128)(2,1)} %broadcast_in_dim.59), calls=%async_computation.13 | async-start | bytes 1048576 | tf_op jit(solution)/shard_map/all_to_all | solution.py:24
  267.8 10.3 %all-to-all-start.15 = ((f32[16,8,128]{2,1,0:T(8,128)}), f32[16,8,128]{2,1,0:T(8,128)S(1)}, u32[]{:S(2)}, u32[]{:S(2)}) async-start(f32[16,8,128]{2,1,0:T(8,128)} %broadcast_in_dim.61), calls=%async_computation.15 | async-start | bytes 131072 | tf_op jit(solution)/shard_map/all_to_all | solution.py:24
  278.1 11.0 %all-to-all-start.14 = ((f32[8,8,1024]{2,1,0:T(8,128)}), f32[8,8,1024]{2,1,0:T(8,128)S(1)}, u32[]{:S(2)}, u32[]{:S(2)}) async-start(f32[8,8,1024]{2,1,0:T(8,128)} %fusion.45), calls=%async_computation.14 | async-start | bytes 524288 | tf_op jit(solution)/shard_map/all_to_all | solution.py:40
  312.0 9.8 %all-to-all-start.17 = ((f32[16,8,256]{2,1,0:T(8,128)}), f32[16,8,256]{2,1,0:T(8,128)S(1)}, u32[]{:S(2)}, u32[]{:S(2)}) async-start(f32[16,8,256]{2,1,0:T(8,128)} %convolution_bitcast_fusion.1), calls=%async_computation.17 | async-start | bytes 262144 | tf_op jit(solution)/shard_map/all_to_all | solution.py:40
  322.5 9.7 %all-to-all-start.18 = ((bf16[16,8,256]{2,1,0:T(8,128)(2,1)}), bf16[16,8,256]{2,1,0:T(8,128)(2,1)S(1)}, u32[]{:S(2)}, u32[]{:S(2)}) async-start(bf16[16,8,256]{2,1,0:T(8,128)(2,1)} %broadcast_in_dim.63), calls=%async_computation.18 | async-start | bytes 131072 | tf_op jit(solution)/shard_map/all_to_all | solution.py:24
  333.4 14.2 %all-to-all-start.19 = ((bf16[8,8,4096]{2,1,0:T(8,128)(2,1)}), bf16[8,8,4096]{2,1,0:T(8,128)(2,1)S(1)}, u32[]{:S(2)}, u32[]{:S(2)}) async-start(bf16[8,8,4096]{2,1,0:T(8,128)(2,1)} %broadcast_in_dim.65), calls=%async_computation.19 | async-start | bytes 1048576 | tf_op jit(solution)/shard_map/all_to_all | solution.py:24
  348.2 10.3 %all-to-all-start.21 = ((f32[16,8,128]{2,1,0:T(8,128)}), f32[16,8,128]{2,1,0:T(8,128)S(1)}, u32[]{:S(2)}, u32[]{:S(2)}) async-start(f32[16,8,128]{2,1,0:T(8,128)} %broadcast_in_dim.67), calls=%async_computation.21 | async-start | bytes 131072 | tf_op jit(solution)/shard_map/all_to_all | solution.py:24
  358.5 11.0 %all-to-all-start.20 = ((f32[8,8,1024]{2,1,0:T(8,128)}), f32[8,8,1024]{2,1,0:T(8,128)S(1)}, u32[]{:S(2)}, u32[]{:S(2)}) async-start(f32[8,8,1024]{2,1,0:T(8,128)} %fusion.43), calls=%async_computation.20 | async-start | bytes 524288 | tf_op jit(solution)/shard_map/all_to_all | solution.py:40
  (4 other events, 40.0 us)
Sparse Core Ops, SparseCore 0:
  10.5 86.1 all-gather.1
where the time goes:
time: 416 us; the launch traced here: 413 us
  waiting for transfers between devices  128 us (31%)
  starting transfers between devices  87.5 us (21%)
  local copies, waits for them, and re-layouts  58.5 us (14%)
  matrix products  50.9 us (12%)
  blocking collectives  39.2 us (9%)
  other arithmetic  34.5 us (8%)
  between operations  14.6 us (4%)
    all_to_all x12, waiting for transfers between devices, copy_for_each(): lax.all_to_all(jnp.broadcast_to(value[None], (devices, *value.shape)), ax...  73.2 us
    all_to_all x12, starting transfers between devices, copy_for_each(): lax.all_to_all(jnp.broadcast_to(value[None], (devices, *value.shape)), ax...  51.8 us
    all_to_all x7, waiting for transfers between devices, sent_and_summed(): lax.all_to_all(cut_along(value, dim, devices), axis, 0, 0, tiled=True)  46.2 us
    all_to_all x3, blocking collectives, copy_for_each(): lax.all_to_all(jnp.broadcast_to(value[None], (devices, *value.shape)), ax...  30.2 us
    all_to_all x7, starting transfers between devices, sent_and_summed(): lax.all_to_all(cut_along(value, dim, devices), axis, 0, 0, tiled=True)  28.3 us
    dot_general x4, matrix products, body(): jnp.einsum('rhpn,rn->rhp', state, c_group, precision=lax.Precision.HIGHEST)  28.2 us
    unnamed x33, local copies, waits for them, and re-layouts  23 us
    dot_general x4, matrix products, body(): partial_value = jnp.dot(scaled, new_out, preferred_element_type=jnp.float32)  15.5 us
  transfers between devices with their start and end apart: 21, of which 19 were waited for; matrix products, arithmetic and copies ran while one was open for 17% of the time, Pallas kernels for 0%

commit v1 on v0

v1 whole, which is shorter than its diff:
```python
import functools

import jax
import jax.numpy as jnp
from jax import lax
from jax.experimental import pallas as pl
from jax.experimental.pallas import tpu as pltpu
from jax.sharding import PartitionSpec as P

H = 128
G = 4
BLK = 128
STEPS = 4
DI = 8192
D = 4096
EPS = 1e-05
DP = 8
TP = 16
ROWS = 64
R = 8
F = D // DP
C = DI // TP
N = 256
HEADS = H // TP
PS = 64
PEERS = TP // G
NZ = 2 * C + 2 * N + 128
NQ = C + 128
SLAB = F + 48

BF = jnp.bfloat16
F32 = jnp.float32
VM = pl.BlockSpec(memory_space=pltpu.VMEM)
SM = pl.BlockSpec(memory_space=pltpu.SMEM)
PARAMS = pltpu.CompilerParams(vmem_limit_bytes=20 * 2**20)


def split_pair(value):
    high = value.astype(BF).astype(F32)
    return high, value - high


def lanes(rows):
    return lax.broadcasted_iota(jnp.int32, (rows, 128), 1)


def project(x, gain_ref, w_ref, out_ref):
    v = (x * gain_ref[...]).astype(BF)
    squares = jnp.sum(x * x, axis=-1, keepdims=True)
    zx = jnp.dot(v, w_ref[...], preferred_element_type=F32)
    high, low = split_pair(squares)
    spot = lanes(ROWS)
    last = zx[:, NZ - 128 :]
    last = jnp.where(spot == HEADS, high, jnp.where(spot == HEADS + 1, low, last))
    out_ref[:, : NZ - 128] = zx[:, : NZ - 128].astype(BF)
    out_ref[:, NZ - 128 : NZ] = last.astype(BF)


def first_kernel(hid_ref, gain_ref, w_ref, out_ref):
    project(hid_ref[...].astype(F32), gain_ref, w_ref, out_ref)


def group_sum(parts_ref, first, rows):
    total = jnp.zeros((rows, parts_ref.shape[2] - 128), F32)
    for g in range(G):
        part = jnp.zeros_like(total)
        pair = jnp.zeros((rows, 128), F32)
        for k in range(PEERS):
            slab = parts_ref[first + g * PEERS + k].astype(F32)
            part = part + slab[:, :-128]
            pair = pair + slab[:, -128:]
        squares = pair[:, 0:1] + pair[:, 1:2]
        total = total + part * lax.rsqrt(squares / (DI // G) + EPS)
    return total


def next_kernel(parts_ref, hid_ref, gain_ref, w_ref, out_ref):
    mixed = group_sum(parts_ref, 0, ROWS).astype(BF)
    out_ref[:, NZ:] = mixed
    project(hid_ref[...].astype(F32) + mixed.astype(F32), gain_ref, w_ref, out_ref)


def silu(value):
    return value / (1.0 + jnp.exp(-value))


def state_kernel(
    has_mixed,
    where_ref,
    zx_ref,
    hx0_ref,
    hx1_ref,
    hx2_ref,
    hb0_ref,
    hb1_ref,
    hb2_ref,
    cx_ref,
    cb_ref,
    head_ref,
    gain_ref,
    state_ref,
    out_ref,
    inner_ref,
    bc_ref,
    new_ref,
    *rest,
):
    if has_mixed:
        mixed_ref, xt_ref, dt_ref, rd_ref = rest
    else:
        xt_ref, dt_ref, rd_ref = rest
    z = zx_ref[0][:, :NZ].astype(F32)
    for k in range(1, DP):
        z = z + zx_ref[k][:, :NZ].astype(F32)
    tail = z[:, NZ - 128 :]
    squares = tail[:, HEADS : HEADS + 1] + tail[:, HEADS + 1 : HEADS + 2]
    z = z * lax.rsqrt(squares / D + EPS)
    gate = z[:, :C]
    inner = z[:, C : 2 * C]
    bc = z[:, 2 * C : 2 * C + 2 * N]
    inner_ref[...] = inner
    bc_ref[...] = bc
    conv_x = silu(
        hx0_ref[...] * cx_ref[0:1]
        + hx1_ref[...] * cx_ref[1:2]
        + hx2_ref[...] * cx_ref[2:3]
        + inner * cx_ref[3:4]
        + cx_ref[4:5]
    )
    conv_bc = silu(
        hb0_ref[...] * cb_ref[0:1]
        + hb1_ref[...] * cb_ref[1:2]
        + hb2_ref[...] * cb_ref[2:3]
        + bc * cb_ref[3:4]
        + cb_ref[4:5]
    )
    spot = lanes(R)
    raw = jnp.concatenate(
        [
            jnp.where(
                spot < PS,
                z[:, NZ - 128 + 2 * j : NZ - 128 + 2 * j + 1],
                z[:, NZ - 128 + 2 * j + 1 : NZ - 128 + 2 * j + 2],
            )
            for j in range(HEADS // 2)
        ],
        axis=1,
    )
    raw = raw + head_ref[0:1]
    step_size = jnp.maximum(raw, 0.0) + jnp.log1p(jnp.exp(-jnp.abs(raw)))
    decay = jnp.exp(-step_size * head_ref[1:2])
    xt_ref[:, :R] = (step_size * conv_x).T
    dt_ref[:, :R] = decay.T

    def one_head(h, carry):
        span = pl.ds(pl.multiple_of(h * PS, PS), PS)
        for r in range(R):
            fresh = dt_ref[span, r : r + 1] * state_ref[r, h] + xt_ref[span, r : r + 1] * conv_bc[r : r + 1, :N]
            new_ref[r, h] = fresh
            rd_ref[span, r : r + 1] = jnp.sum(fresh * conv_bc[r : r + 1, N:], axis=-1, keepdims=True)
        return carry

    lax.fori_loop(0, HEADS, one_head, 0)
    read = rd_ref[:, :R].T + head_ref[2:3] * conv_x
    gated = read * silu(gate)
    high, low = split_pair(jnp.sum(gated * gated, axis=-1, keepdims=True))
    message = (gated * gain_ref[...]).astype(BF)
    pair = jnp.where(spot == 0, high, jnp.where(spot == 1, low, 0.0)).astype(BF)
    for k in range(DP):
        out_ref[k, :, :C] = message
        out_ref[k, :, C:] = pair
    if has_mixed:
        slot = where_ref[1]
        half = pl.multiple_of(NZ + lax.rem(slot, 2) * 256, 128)
        mixed_ref[...] = zx_ref[slot // 2, :, pl.ds(half, 256)]


def out_kernel(q_ref, w_ref, out_ref):
    part = jnp.dot(q_ref[:, :C], w_ref[...], preferred_element_type=F32).astype(BF)
    pair = q_ref[:, C:]
    for k in range(TP):
        out_ref[k, :, :C] = part
        out_ref[k, :, C:] = pair


def last_kernel(where_ref, q_ref, w_ref, out_ref):
    part = jnp.dot(q_ref[:, :C], w_ref[...], preferred_element_type=F32).astype(BF)
    pair = q_ref[:, C:]
    out_ref[...] = jnp.zeros_like(out_ref)
    me = where_ref[0]
    for k in range(DP):
        for half in range(2):
            slot = k * TP + 2 * me + half
            out_ref[slot, :, :256] = part[k * R : k * R + R, half * 256 : half * 256 + 256]
            out_ref[slot, :, 256:] = pair[k * R : k * R + R]


def finish_kernel(where_ref, parts_ref, out_ref):
    out_ref[...] = group_sum(parts_ref, (where_ref[1] // 2) * TP, R).astype(BF)


def struct(shape, dtype):
    return jax.ShapeDtypeStruct(shape, dtype)


def call(kernel, outs, operands, **extra):
    return pl.pallas_call(
        kernel,
        out_shape=outs,
        in_specs=[SM if o.dtype == jnp.int32 else VM for o in operands],
        out_specs=jax.tree.map(lambda _: VM, outs),
        compiler_params=PARAMS,
        **extra,
    )(*operands)


def swap(value, axis):
    return lax.all_to_all(value, axis, 0, 0, tiled=True)


def decode_pairs(codes, exponents, block):
    rows, pair, cols = codes.shape
    blocked = codes.astype(jnp.float32).reshape(rows // block, block, pair, cols // block, block)
    scales = jnp.exp2(exponents.astype(jnp.float32))
    return (blocked * scales[:, None, :, :, None]).reshape(rows, pair, cols)


def decode_matrix(codes, exponents, block):
    rows, cols = codes.shape
    blocked = codes.astype(jnp.float32).reshape(rows // block, block, cols // block, block)
    scales = jnp.exp2(exponents.astype(jnp.float32))
    return (blocked * scales[:, None, :, None]).reshape(rows, cols)


def group_parameters(w_bc_rows, conv_bc, conv_state_bc, slot):
    high = conv_bc.astype(BF)
    rest = conv_bc - high.astype(F32)
    mid = rest.astype(BF)
    low = (rest - mid.astype(F32)).astype(BF)
    history = jnp.moveaxis(conv_state_bc, 1, 0).reshape(3 * R, 128)
    slab = jnp.concatenate([w_bc_rows, history, high, mid, low, jnp.zeros((SLAB - F - 39, 128), BF)], 0)
    needed = [[2 * g, 2 * g + 1, 8 + 2 * g, 9 + 2 * g] for g in range(G)]
    got = []
    for turn in range(PEERS):
        pairs = [(needed[g][(i + turn) % PEERS], g * PEERS + i) for g in range(G) for i in range(PEERS)]
        got.append(lax.ppermute(slab, "tp", pairs))
    first = (PEERS - slot % PEERS) % PEERS
    wide = jnp.stack(got + got)
    mine = lax.dynamic_slice_in_dim(wide, first, PEERS, 0)
    whole = jnp.moveaxis(mine, 0, 1).reshape(SLAB, 2 * N)
    taps = whole[F + 24 : F + 39].astype(F32)
    return whole[:F], whole[F : F + 24].astype(F32), taps[0:5] + taps[5:10] + taps[10:15]


def body(
    hidden_in,
    pre_gain,
    w_zx,
    zx_codes,
    zx_exponents,
    w_bc,
    w_dt,
    conv_x,
    conv_bc,
    dt_bias,
    decay_rate,
    skip_gain,
    conv_state_x,
    conv_state_bc,
    ssm_state,
    norm_gain,
    w_out,
    out_codes,
    out_exponents,
):
    replica = lax.axis_index("dp")
    slot = lax.axis_index("tp")
    where = jnp.stack([replica, slot]).astype(jnp.int32)

    traded = lax.all_to_all(zx_codes, "tp", split_axis=2, concat_axis=0, tiled=True)
    hid = swap(jnp.moveaxis(hidden_in.reshape(STEPS, R, DP, F), 2, 0), "dp")
    hid = jnp.moveaxis(hid, 1, 0).reshape(STEPS, ROWS, F)
    w_bc_rows = lax.dynamic_slice_in_dim(w_bc, replica * F, F, 0)
    bc_weights, history_bc, taps_bc = group_parameters(w_bc_rows, conv_bc, conv_state_bc, slot)

    w_rows = lax.dynamic_slice_in_dim(w_zx, replica * F, F, 0)
    zx_weights = (
        (w_rows.astype(F32) + decode_pairs(traded, zx_exponents, BLK)).astype(BF).reshape(F, 2 * C)
    )
    dt_rows = jnp.pad(lax.dynamic_slice_in_dim(w_dt, replica * F, F, 0), ((0, 0), (0, 128 - HEADS)))
    weights = jnp.concatenate([zx_weights, bc_weights, dt_rows], 1)
    w_out_cols = lax.dynamic_slice_in_dim(w_out, replica * 512, 512, 1)
    out_weights = (w_out_cols.astype(F32) + decode_matrix(out_codes, out_exponents, BLK)).astype(BF)

    gain = lax.dynamic_slice_in_dim(pre_gain, replica * F, F, 0)[None]
    head = jnp.repeat(jnp.stack([dt_bias, decay_rate, skip_gain]), PS, axis=1)
    norm = norm_gain[None]
    hx = [conv_state_x[:, k].astype(F32) for k in range(3)]
    hb = [history_bc[k * R : k * R + R] for k in range(3)]
    state = ssm_state
    results = []
    parts = None
    for step in range(STEPS):
        if step == 0:
            zx = call(first_kernel, struct((ROWS, NZ), BF), [hid[0], gain, weights])
        else:
            zx = call(next_kernel, struct((ROWS, NZ + 512), BF), [parts, hid[step], gain, weights])
        zx = swap(zx.reshape(DP, R, -1), "dp")
        outs = [
            struct((DP, R, NQ), BF),
            struct((R, C), F32),
            struct((R, 2 * N), F32),
            struct(state.shape, F32),
        ]
        if step > 0:
            outs.append(struct((R, 256), BF))
        got = call(
            functools.partial(state_kernel, step > 0),
            outs,
            [where, zx, *hx, *hb, conv_x, taps_bc, head, norm, state],
            scratch_shapes=[pltpu.VMEM((C, 128), F32)] * 3,
            input_output_aliases={12: 3} if step else {},
        )
        q, inner, bc, state = got[:4]
        if step > 0:
            results.append(got[4])
        hx = hx[1:] + [inner]
        hb = hb[1:] + [bc]
        q = swap(q, "dp").reshape(ROWS, NQ)
        if step + 1 < STEPS:
            parts = swap(call(out_kernel, struct((TP, ROWS, NQ), BF), [q, out_weights]), "tp")
        else:
            tiles = call(last_kernel, struct((DP * TP, R, 384), BF), [where, q, out_weights])
            tiles = lax.all_to_all(tiles, ("dp", "tp"), 0, 0, tiled=True)
            results.append(call(finish_kernel, struct((R, 256), BF), [where, tiles]))
    return (jnp.stack(results), state)


def solution(mesh):
    return jax.shard_map(
        body,
        mesh=mesh,
        in_specs=(
            P(None, "dp", None),
            P(),
            P(None, None, "tp"),
            P(("dp", "tp"), None, None),
            P("dp", None, "tp"),
            P(None, "tp"),
            P(None, "tp"),
            P(None, "tp"),
            P(None, "tp"),
            P("tp"),
            P("tp"),
            P("tp"),
            P("dp", None, "tp"),
            P("dp", None, "tp"),
            P("dp", "tp", None, None),
            P("tp"),
            P("tp", None),
            P("tp", "dp"),
            P("tp", "dp"),
        ),
        out_specs=(P(None, "dp", "tp"), P("dp", "tp", None, None)),
        check_vma=False,
    )
```

time: 416 us -> 319 us (0.77)
  blocking collectives: 39.2 us -> 155 us
  waiting for transfers between devices: 128 us -> 26.8 us
  starting transfers between devices: 87.5 us -> 31 us
  matrix products: 50.9 us -> 0 us
  Pallas kernels: 0 us -> 45.3 us
  other arithmetic: 34.5 us -> 15.4 us
  local copies, waits for them, and re-layouts: 58.5 us -> 43.4 us
  between operations: 14.6 us -> 1.11 us
    all_to_all x4 -> x10, blocking collectives: 39.2 us -> 155 us  [the longest x9 132 us: swap(): return lax.all_to_all(value, axis, 0, 0, tiled=True)]
    all_to_all x19 -> x3, waiting for transfers between devices: 119 us -> 12 us  [swap(): return lax.all_to_all(value, axis, 0, 0, tiled=True)]
    all_to_all x19 -> x3, starting transfers between devices: 80.2 us -> 17.3 us  [swap(): return lax.all_to_all(value, axis, 0, 0, tiled=True)]
    dot_general x20 -> x0, matrix products: 50.9 us -> none  [the longest x4 28.2 us: body(): jnp.einsum('rhpn,rn->rhp', state, c_group, precision=lax.Precision.HIGHEST)]
    pallas_call x0 -> x13, Pallas kernels: none -> 45.3 us  [call(): pl.pallas_call(kernel, out_shape=outs, in_specs=[SM if o.dtype == jnp.int...]
    ppermute x0 -> x4, starting transfers between devices: none -> 9.12 us  [group_parameters(): got.append(lax.ppermute(slab, 'tp', pairs))]
    broadcast_in_dim x15 -> x2, local copies, waits for them, and re-layouts: 8.41 us -> 0.07 us  [the longest x1 0.07 us: body(): head = jnp.repeat(jnp.stack([dt_bias, decay_rate, skip_gain]), PS, axis=1)]
    dot_general x1 -> x0, other arithmetic: 7.26 us -> none  [body(): partial_value = jnp.dot(scaled, new_out, preferred_element_type=jnp.float32)]
  transfers between devices with their start and end apart: 21 -> 8, of which waited for: 19 -> 3; matrix products, arithmetic and copies ran while one was open for 17% -> 8% of each run, Pallas kernels for 0% -> 0%
where the time goes in v1:
time: 319 us; the launch traced here: 318 us
  blocking collectives  155 us (49%)
  Pallas kernels  45.3 us (14%)
  local copies, waits for them, and re-layouts  43.4 us (14%)
  starting transfers between devices  31 us (10%)
  waiting for transfers between devices  26.8 us (8%)
  other arithmetic  15.4 us (5%)
    all_to_all x9, blocking collectives, swap(): return lax.all_to_all(value, axis, 0, 0, tiled=True)  132 us
    pallas_call x13, Pallas kernels, call(): pl.pallas_call(kernel, out_shape=outs, in_specs=[SM if o.dtype == jnp.int...  45.3 us
    unnamed x39, local copies, waits for them, and re-layouts  25.7 us
    all_to_all x1, blocking collectives, body(): tiles = lax.all_to_all(tiles, ('dp', 'tp'), 0, 0, tiled=True)  22.7 us
    all_to_all x3, starting transfers between devices, swap(): return lax.all_to_all(value, axis, 0, 0, tiled=True)  17.3 us
    all_to_all x1, waiting for transfers between devices, body(): lax.all_to_all(zx_codes, 'tp', split_axis=2, concat_axis=0, tiled=True)  14.9 us
    all_to_all x3, waiting for transfers between devices, swap(): return lax.all_to_all(value, axis, 0, 0, tiled=True)  12 us
    convert_element_type x1, local copies, waits for them, and re-layouts, decode_pairs(): codes.astype(jnp.float32)  10.3 us
  transfers between devices with their start and end apart: 8, of which 3 were waited for; matrix products, arithmetic and copies ran while one was open for 8% of the time, Pallas kernels for 0%

profile of v1, /device:TPU:1, one launch (start us, length us, event | category | flops | bytes accessed | tf_op | source)
XLA Modules:
  0.0 317.8 jit_solution(1039314785476515823)
XLA Ops:
  5.0 5.5 %collective-permute-start.2 = (bf16[560,128]{1,0:T(8,128)(2,1)S(1)}, bf16[560,128]{1,0:T(8,128)(2,1)S(1)}, u32[]{:S(2)}, u32[]{:S(2)}) collective-permute-start(bf16[560,128]{1,0:T(8,128)(2,1)S(1)} %concatenate.6), channel_id=1, source_target_pairs={{8,0},{9,1},{0,2},{1,3},{10,4},{11,5},{2,6},{3,7},{12,8},{13,9},{4... | collective-permute-start | bytes 430088 | tf_op jit(solution)/shard_map/ppermute | solution.py:246
  10.5 1.5 collective-permute-start.3
  13.8 7.0 %all-to-all-start = ((bf16[8,4,8,512]{3,2,1,0:T(8,128)(2,1)}), bf16[8,4,8,512]{3,2,1,0:T(8,128)(2,1)S(1)}, u32[]{:S(2)}, u32[]{:S(2)}) async-start(bf16[8,4,8,512]{3,2,1,0:T(8,128)(2,1)} %copy.36), calls=%async_computation | async-start | bytes 524288 | tf_op jit(solution)/shard_map/all_to_all | solution.py:218
  21.7 7.4 %copy.37 = bf16[32,2,8192]{0,1,2:T(2,128)(2,1)} copy(bf16[32,2,8192]{2,1,0:T(2,128)(2,1)S(1)} %copy-done.6) | data formatting | bytes 2097152 | tf_op args[3]
  29.1 9.9 %reshape.100 = bf16[16,2,16384]{2,1,0:T(2,128)(2,1)} reshape(bf16[8192,2,32]{2,1,0:T(2,128)(2,1)} %bitcast.118) | data formatting | bytes 2097152
  39.4 2.6 mul.31
  43.4 4.6 %all-to-all-start.1 = ((bf16[16,2,16384]{2,1,0:T(2,128)(2,1)}), bf16[16,2,16384]{2,1,0:T(2,128)(2,1)S(1)}, u32[]{:S(2)}, u32[]{:S(2)}) async-start(bf16[16,2,16384]{2,1,0:T(2,128)(2,1)} %reshape.100), calls=%async_computation.1 | async-start | bytes 2097152 | tf_op jit(solution)/shard_map/all_to_all | solution.py:280
  48.9 14.9 %all-to-all-done.1 = bf16[16,2,16384]{2,1,0:T(2,128)(2,1)S(1)} async-done(((bf16[16,2,16384]{2,1,0:T(2,128)(2,1)}), bf16[16,2,16384]{2,1,0:T(2,128)(2,1)S(1)}, u32[]{:S(2)}, u32[]{:S(2)}) %all-to-all-start.1) | async-done | bytes 1048608 | tf_op jit(solution)/shard_map/all_to_all | solution.py:280
  63.8 3.5 %reshape.101 = bf16[8192,2,32]{2,1,0:T(2,128)(2,1)} reshape(bf16[16,2,16384]{2,1,0:T(2,128)(2,1)S(1)} %all-to-all-done.1) | data formatting | bytes 2097152
  67.2 8.9 %convert_bitcast_fusion = f32[16,32,2,512]{1,2,3,0:T(2,128)} fusion(bf16[32,2,16,512]{0,1,3,2:T(2,128)(2,1)} %bitcast.117), kind=kLoop, calls=%fused_computation | loop fusion | flops 524288 | bytes 3145728 | tf_op jit(solution)/shard_map/convert_element_type | solution.py:223
  76.2 10.3 %copy.38 = f32[16,32,2,512]{3,2,1,0:T(2,128)S(1)} copy(f32[16,32,2,512]{1,2,3,0:T(2,128)} %convert_bitcast_fusion) | data formatting | bytes 4194304 | tf_op jit(solution)/shard_map/convert_element_type | solution.py:223
  86.5 3.3 %fusion.2 = bf16[512,2,512]{2,1,0:T(2,128)(2,1)S(1)} fusion(f32[512,2,512]{2,1,0:T(2,128)} %mul.31, f32[16,32,2,512]{3,2,1,0:T(2,128)S(1)} %copy.38, bf16[4096,2,512]{2,1,0:T(2,128)(2,1)} %param.21, s32[]{:T(128)S(6)} %select_n.21), kind=kLoop, calls=%fused_computation.5 | loop fusion | flops 2097152 | bytes 6291460 | tf_op jit(solution)/shard_map/convert_element_type | solution.py:288
  92.1 6.9 %all-to-all-start.2 = ((bf16[8,8,1664]{2,1,0:T(8,128)(2,1)}), bf16[8,8,1664]{2,1,0:T(8,128)(2,1)S(1)}, u32[]{:S(2)}, u32[]{:S(2)}) async-start(bf16[8,8,1664]{2,1,0:T(8,128)(2,1)} %bitcast.16), calls=%async_computation.2 | async-start | bytes 425984 | tf_op jit(solution)/shard_map/all_to_all | solution.py:218
  99.1 7.1 %all-to-all-done.2.zx_ref = bf16[8,8,1664]{2,1,0:T(8,128)(2,1)S(1)} async-done(((bf16[8,8,1664]{2,1,0:T(8,128)(2,1)}), bf16[8,8,1664]{2,1,0:T(8,128)(2,1)S(1)}, u32[]{:S(2)}, u32[]{:S(2)}) %all-to-all-start.2) | async-done | bytes 213024 | tf_op jit(solution)/shard_map/all_to_all | solution.py:218
  106.2 2.2 copy-done.2
  108.3 8.8 %shard_map.195 = (bf16[8,8,640]{2,1,0:T(8,128)(2,1)}, f32[8,512]{1,0:T(8,128)S(1)}, f32[8,512]{1,0:T(8,128)S(1)}, f32[8,8,64,256]{3,2,1,0:T(8,128)}) custom-call(s32[2]{0:T(128)S(1)} %pad_add_fusion.where_ref, bf16[8,8,1664]{2,1,0:T(8,128)(2,1)S(1)} %all-to-all-done.2.zx_ref, f32[8,512]{1,0:T(8,128)S(1)} %get-tuple-element.44.hx0_ref, ...), custom_call_target="tpu_custom_call" | custom-call | tf_op jit(solution)/shard_map/pallas_call | solution.py:207
  117.2 3.4 %all-to-all-start.3 = ((bf16[8,8,640]{2,1,0:T(8,128)(2,1)}), bf16[8,8,640]{2,1,0:T(8,128)(2,1)S(1)}, u32[]{:S(2)}, u32[]{:S(2)}) async-start(bf16[8,8,640]{2,1,0:T(8,128)(2,1)} %get-tuple-element.19), calls=%async_computation.3 | async-start | bytes 163840 | tf_op jit(solution)/shard_map/all_to_all | solution.py:218
  120.8 1.5 fusion.5.w_ref
  122.2 4.9 %all-to-all-done.3 = bf16[8,8,640]{2,1,0:T(8,128)(2,1)S(1)} async-done(((bf16[8,8,640]{2,1,0:T(8,128)(2,1)}), bf16[8,8,640]{2,1,0:T(8,128)(2,1)S(1)}, u32[]{:S(2)}, u32[]{:S(2)}) %all-to-all-start.3) | async-done | bytes 81952 | tf_op jit(solution)/shard_map/all_to_all | solution.py:218
  127.4 24.3 %all_to_all.74.parts_ref = bf16[16,64,640]{2,1,0:T(8,128)(2,1)S(1)} all-to-all(bf16[16,64,640]{2,1,0:T(8,128)(2,1)S(1)} %shard_map.196), channel_id=1, replica_groups=mesh['dp'=8,'tp'=16] {'tp'}, dimensions={0} | all-to-all | bytes 2621440 | tf_op jit(solution)/shard_map/all_to_all | solution.py:218
  152.3 10.7 %all_to_all.75.zx_ref = bf16[8,8,2176]{2,1,0:T(8,128)(2,1)S(1)} all-to-all(bf16[8,8,2176]{2,1,0:T(8,128)(2,1)S(1)} %bitcast.99), channel_id=1, replica_groups=mesh['dp'=8,'tp'=16] {'dp'}, dimensions={0} | all-to-all | bytes 557056 | tf_op jit(solution)/shard_map/all_to_all | solution.py:218
  163.1 10.4 %shard_map.198 = (bf16[8,8,640]{2,1,0:T(8,128)(2,1)S(1)}, f32[8,512]{1,0:T(8,128)S(1)}, f32[8,512]{1,0:T(8,128)S(1)}, f32[8,8,64,256]{3,2,1,0:T(8,128)}, bf16[8,256]{1,0:T(8,128)(2,1)S(1)}) custom-call(s32[2]{0:T(128)S(1)} %pad_add_fusion.where_ref, bf16[8,8,2176]{2,1,0:T(8,128)(2,1)S(1)} %all_to_all.75.zx_ref, ...), custom_call_target="tpu_custom_call", output_to_operand_aliasing={{3}: (12, {})} | custom-call | tf_op jit(solution)/shard_map/pallas_call | solution.py:207
  173.4 9.0 %all_to_all.76 = bf16[8,8,640]{2,1,0:T(8,128)(2,1)S(1)} all-to-all(bf16[8,8,640]{2,1,0:T(8,128)(2,1)S(1)} %get-tuple-element.24), channel_id=1, replica_groups=mesh['dp'=8,'tp'=16] {'dp'}, dimensions={0} | all-to-all | bytes 163840 | tf_op jit(solution)/shard_map/all_to_all | solution.py:218
  182.7 24.2 %all_to_all.77.parts_ref = bf16[16,64,640]{2,1,0:T(8,128)(2,1)S(1)} all-to-all(bf16[16,64,640]{2,1,0:T(8,128)(2,1)S(1)} %shard_map.199), channel_id=1, replica_groups=mesh['dp'=8,'tp'=16] {'tp'}, dimensions={0} | all-to-all | bytes 2621440 | tf_op jit(solution)/shard_map/all_to_all | solution.py:218
  207.5 10.8 %all_to_all.78.zx_ref = bf16[8,8,2176]{2,1,0:T(8,128)(2,1)S(1)} all-to-all(bf16[8,8,2176]{2,1,0:T(8,128)(2,1)S(1)} %bitcast.100), channel_id=1, replica_groups=mesh['dp'=8,'tp'=16] {'dp'}, dimensions={0} | all-to-all | bytes 557056 | tf_op jit(solution)/shard_map/all_to_all | solution.py:218
  218.4 10.4 %shard_map.201 = (bf16[8,8,640]{2,1,0:T(8,128)(2,1)S(1)}, f32[8,512]{1,0:T(8,128)S(1)}, f32[8,512]{1,0:T(8,128)S(1)}, f32[8,8,64,256]{3,2,1,0:T(8,128)}, bf16[8,256]{1,0:T(8,128)(2,1)S(1)}) custom-call(s32[2]{0:T(128)S(1)} %pad_add_fusion.where_ref, bf16[8,8,2176]{2,1,0:T(8,128)(2,1)S(1)} %all_to_all.78.zx_ref, ...), custom_call_target="tpu_custom_call", output_to_operand_aliasing={{3}: (12, {})} | custom-call | tf_op jit(solution)/shard_map/pallas_call | solution.py:207
  228.8 9.0 %all_to_all.79 = bf16[8,8,640]{2,1,0:T(8,128)(2,1)S(1)} all-to-all(bf16[8,8,640]{2,1,0:T(8,128)(2,1)S(1)} %get-tuple-element.29), channel_id=1, replica_groups=mesh['dp'=8,'tp'=16] {'dp'}, dimensions={0} | all-to-all | bytes 163840 | tf_op jit(solution)/shard_map/all_to_all | solution.py:218
  238.1 24.4 %all_to_all.80.parts_ref = bf16[16,64,640]{2,1,0:T(8,128)(2,1)S(1)} all-to-all(bf16[16,64,640]{2,1,0:T(8,128)(2,1)S(1)} %shard_map.202), channel_id=1, replica_groups=mesh['dp'=8,'tp'=16] {'tp'}, dimensions={0} | all-to-all | bytes 2621440 | tf_op jit(solution)/shard_map/all_to_all | solution.py:218
  263.1 10.5 %all_to_all.81.zx_ref = bf16[8,8,2176]{2,1,0:T(8,128)(2,1)S(1)} all-to-all(bf16[8,8,2176]{2,1,0:T(8,128)(2,1)S(1)} %bitcast.98), channel_id=1, replica_groups=mesh['dp'=8,'tp'=16] {'dp'}, dimensions={0} | all-to-all | bytes 557056 | tf_op jit(solution)/shard_map/all_to_all | solution.py:218
  273.6 10.4 %shard_map.204 = (bf16[8,8,640]{2,1,0:T(8,128)(2,1)S(1)}, f32[8,512]{1,0:T(8,128)}, f32[8,512]{1,0:T(8,128)}, f32[8,8,64,256]{3,2,1,0:T(8,128)}, bf16[8,256]{1,0:T(8,128)(2,1)S(1)}) custom-call(s32[2]{0:T(128)S(1)} %pad_add_fusion.where_ref, bf16[8,8,2176]{2,1,0:T(8,128)(2,1)S(1)} %all_to_all.81.zx_ref, ...), custom_call_target="tpu_custom_call", output_to_operand_aliasing={{3}: (12, {})} | custom-call | tf_op jit(solution)/shard_map/pallas_call | solution.py:207
  284.0 9.0 %all_to_all.82 = bf16[8,8,640]{2,1,0:T(8,128)(2,1)S(1)} all-to-all(bf16[8,8,640]{2,1,0:T(8,128)(2,1)S(1)} %get-tuple-element.34), channel_id=1, replica_groups=mesh['dp'=8,'tp'=16] {'dp'}, dimensions={0} | all-to-all | bytes 163840 | tf_op jit(solution)/shard_map/all_to_all | solution.py:218
  293.8 22.7 %all_to_all.83.parts_ref = bf16[128,8,384]{2,1,0:T(8,128)(2,1)S(1)} all-to-all(bf16[128,8,384]{2,1,0:T(8,128)(2,1)S(1)} %shard_map.205), channel_id=1, replica_groups=mesh['dp'=8,'tp'=16] {'dp','tp'}, dimensions={0} | all-to-all | bytes 1572864 | tf_op jit(solution)/shard_map/all_to_all | solution.py:334
  (77 shorter events, 16.7 us)
Async XLA Ops:
  0.6 1.2 copy-start
  0.7 20.2 %copy-start.8 = (s32[4,2,4]{2,1,0:T(2,128)S(1)}, s32[4,2,4]{2,1,0:T(2,128)}, u32[]{:S(2)}) copy-start(s32[4,2,4]{2,1,0:T(2,128)} %param.23) | copy-start | bytes 388
  0.7 20.9 %copy-start.7 = (bf16[8,3,512]{2,0,1:T(8,128)(2,1)S(1)}, bf16[8,3,512]{2,0,1:T(8,128)(2,1)}, u32[]{:S(2)}) copy-start(bf16[8,3,512]{2,0,1:T(8,128)(2,1)} %param.31) | copy-start | bytes 73732
  0.7 20.9 %copy-start.9 = (s32[4,4]{1,0:T(4,128)S(1)}, s32[4,4]{1,0:T(4,128)}, u32[]{:S(2)}) copy-start(s32[4,4]{1,0:T(4,128)} %param.37) | copy-start | bytes 196
  0.7 20.9 %copy-start.12 = (f32[8]{0:T(128)S(1)}, f32[8]{0:T(128)}, u32[]{:S(2)}) copy-start(f32[8]{0:T(128)} %param.28) | copy-start | bytes 100
  0.7 20.9 %copy-start.11 = (f32[8]{0:T(128)S(1)}, f32[8]{0:T(128)}, u32[]{:S(2)}) copy-start(f32[8]{0:T(128)} %param.29) | copy-start | bytes 100
  0.7 20.9 %copy-start.10 = (f32[8]{0:T(128)S(1)}, f32[8]{0:T(128)}, u32[]{:S(2)}) copy-start(f32[8]{0:T(128)} %param.30) | copy-start | bytes 100
  0.7 21.0 %copy-start.6 = (bf16[32,2,8192]{2,1,0:T(2,128)(2,1)S(1)}, bf16[32,2,8192]{2,1,0:T(2,128)(2,1)}, u32[]{:S(2)}) copy-start(bf16[32,2,8192]{2,1,0:T(2,128)(2,1)} %param.22) | copy-start | bytes 3145732
  2.8 40.3 %collective-permute-start = (bf16[560,128]{1,0:T(8,128)(2,1)S(1)}, bf16[560,128]{1,0:T(8,128)(2,1)S(1)}, u32[]{:S(2)}, u32[]{:S(2)}) collective-permute-start(bf16[560,128]{1,0:T(8,128)(2,1)S(1)} %concatenate.6), channel_id=1, source_target_pairs={{0,0},{1,1},{8,2},{9,3},{2,4},{3,5},{10,6},{11,7},{4,8},{5,9},{12,... | collective-permute-start | bytes 430088 | tf_op jit(solution)/shard_map/ppermute | solution.py:246
  3.5 39.6 %collective-permute-start.1 = (bf16[560,128]{1,0:T(8,128)(2,1)S(1)}, bf16[560,128]{1,0:T(8,128)(2,1)S(1)}, u32[]{:S(2)}, u32[]{:S(2)}) collective-permute-start(bf16[560,128]{1,0:T(8,128)(2,1)S(1)} %concatenate.6), channel_id=1, source_target_pairs={{1,0},{8,1},{9,2},{0,3},{3,4},{10,5},{11,6},{2,7},{5,8},{12,9},{13... | collective-permute-start | bytes 430088 | tf_op jit(solution)/shard_map/ppermute | solution.py:246
  5.0 38.2 %collective-permute-start.2 = (bf16[560,128]{1,0:T(8,128)(2,1)S(1)}, bf16[560,128]{1,0:T(8,128)(2,1)S(1)}, u32[]{:S(2)}, u32[]{:S(2)}) collective-permute-start(bf16[560,128]{1,0:T(8,128)(2,1)S(1)} %concatenate.6), channel_id=1, source_target_pairs={{8,0},{9,1},{0,2},{1,3},{10,4},{11,5},{2,6},{3,7},{12,8},{13,9},{4... | collective-permute-start | bytes 430088 | tf_op jit(solution)/shard_map/ppermute | solution.py:246
  10.5 32.7 %collective-permute-start.3 = (bf16[560,128]{1,0:T(8,128)(2,1)S(1)}, bf16[560,128]{1,0:T(8,128)(2,1)S(1)}, u32[]{:S(2)}, u32[]{:S(2)}) collective-permute-start(bf16[560,128]{1,0:T(8,128)(2,1)S(1)} %concatenate.6), channel_id=1, source_target_pairs={{9,0},{0,1},{1,2},{8,3},{11,4},{2,5},{3,6},{10,7},{13,8},{4,9},{5,... | collective-permute-start | bytes 430088 | tf_op jit(solution)/shard_map/ppermute | solution.py:246
  13.8 29.6 %all-to-all-start = ((bf16[8,4,8,512]{3,2,1,0:T(8,128)(2,1)}), bf16[8,4,8,512]{3,2,1,0:T(8,128)(2,1)S(1)}, u32[]{:S(2)}, u32[]{:S(2)}) async-start(bf16[8,4,8,512]{3,2,1,0:T(8,128)(2,1)} %copy.36), calls=%async_computation | async-start | bytes 524288 | tf_op jit(solution)/shard_map/all_to_all | solution.py:218
  43.4 20.3 %all-to-all-start.1 = ((bf16[16,2,16384]{2,1,0:T(2,128)(2,1)}), bf16[16,2,16384]{2,1,0:T(2,128)(2,1)S(1)}, u32[]{:S(2)}, u32[]{:S(2)}) async-start(bf16[16,2,16384]{2,1,0:T(2,128)(2,1)} %reshape.100), calls=%async_computation.1 | async-start | bytes 2097152 | tf_op jit(solution)/shard_map/all_to_all | solution.py:280
  89.8 1.0 copy-start.5
  91.0 15.1 %copy-start.3 = (f32[5,512]{1,0:T(8,128)S(1)}, f32[5,512]{1,0:T(8,128)}, u32[]{:S(2)}) copy-start(f32[5,512]{1,0:T(8,128)} %cx_ref.7) | copy-start | bytes 30724
  91.0 15.1 %copy-start.4 = (f32[512]{0:T(512)S(1)}, f32[512]{0:T(512)}, u32[]{:S(2)}) copy-start(f32[512]{0:T(512)} %param.34) | copy-start | bytes 6148
  92.1 14.0 %all-to-all-start.2 = ((bf16[8,8,1664]{2,1,0:T(8,128)(2,1)}), bf16[8,8,1664]{2,1,0:T(8,128)(2,1)S(1)}, u32[]{:S(2)}, u32[]{:S(2)}) async-start(bf16[8,8,1664]{2,1,0:T(8,128)(2,1)} %bitcast.16), calls=%async_computation.2 | async-start | bytes 425984 | tf_op jit(solution)/shard_map/all_to_all | solution.py:218
  106.2 2.2 copy-start.2
  117.2 9.9 %all-to-all-start.3 = ((bf16[8,8,640]{2,1,0:T(8,128)(2,1)}), bf16[8,8,640]{2,1,0:T(8,128)(2,1)S(1)}, u32[]{:S(2)}, u32[]{:S(2)}) async-start(bf16[8,8,640]{2,1,0:T(8,128)(2,1)} %get-tuple-element.19), calls=%async_computation.3 | async-start | bytes 163840 | tf_op jit(solution)/shard_map/all_to_all | solution.py:218
  293.0 24.7 %copy-start.1 = (bf16[4096,128]{1,0:T(8,128)(2,1)S(1)}, bf16[4096,128]{1,0:T(8,128)(2,1)}, u32[]{:S(2)}) copy-start(bf16[4096,128]{1,0:T(8,128)(2,1)} %param.24) | copy-start | bytes 3145732

commit v2 on v1

v2 whole, which is shorter than its diff:
```python
import functools

import jax
import jax.numpy as jnp
from jax import lax
from jax.experimental import pallas as pl
from jax.experimental.pallas import tpu as pltpu
from jax.sharding import PartitionSpec as P

H = 128
G = 4
BLK = 128
STEPS = 4
DI = 8192
D = 4096
EPS = 1e-05
DP = 8
TP = 16
ROWS = 64
R = 8
F = D // DP
C = DI // TP
N = 256
HEADS = H // TP
PS = 64
PEERS = TP // G
NZ = 2 * C + 2 * N + 128
NQ = C + 128
SLAB = F + 48

BF = jnp.bfloat16
F32 = jnp.float32
VM = pl.BlockSpec(memory_space=pltpu.VMEM)
HB = pl.BlockSpec(memory_space=pltpu.HBM)
SM = pl.BlockSpec(memory_space=pltpu.SMEM)
PARAMS = pltpu.CompilerParams(vmem_limit_bytes=20 * 2**20)
WHOLE = pltpu.CompilerParams(vmem_limit_bytes=60 * 1024 * 2**10)


def split_pair(value):
    high = value.astype(BF).astype(F32)
    return high, value - high


def lanes(rows):
    return lax.broadcasted_iota(jnp.int32, (rows, 128), 1)


def product(left, right_ref):
    return jnp.dot(left, right_ref[...], preferred_element_type=F32)


def project(x, gain_ref, wz_ref, wbc_ref, wdt_ref, out_ref):
    v = (x * gain_ref[...]).astype(BF)
    high, low = split_pair(jnp.sum(x * x, axis=-1, keepdims=True))
    spot = lanes(ROWS)
    last = product(v, wdt_ref)
    last = jnp.where(spot == HEADS, high, jnp.where(spot == HEADS + 1, low, last))
    out_ref[:, : 2 * C] = product(v, wz_ref).astype(BF)
    out_ref[:, 2 * C : NZ - 128] = product(v, wbc_ref).astype(BF)
    out_ref[:, NZ - 128 : NZ] = last.astype(BF)


def fresh_rows(hid_ref, step):
    return hid_ref[:, step].astype(F32).reshape(ROWS, F)


def first_kernel(hid_ref, *refs):
    project(fresh_rows(hid_ref, 0), *refs)


def pack_kernel(codes_ref, out_ref):
    for k in range(TP):
        out_ref[k] = jnp.transpose(codes_ref[:, :, k * C : k * C + C], (1, 0, 2))


def decode_kernel(codes_ref, w_ref, scale_ref, out_ref):
    depth = F // TP
    for k in range(BLK // depth):
        for pair in range(2):
            row = pl.program_id(0) * 2 + pair
            delta = codes_ref[k, pair].astype(F32) * scale_ref[pl.ds(row, 1)]
            old = w_ref[pair, k * depth : k * depth + depth].astype(F32)
            out_ref[k * depth : k * depth + depth, pair * C : pair * C + C] = (old + delta).astype(BF)


def slab_kernel(where_ref, w_hbm, taps_ref, history_ref, out_ref, w_ref, sem):
    first = pl.multiple_of(where_ref[0] * F, F)
    copy = pltpu.make_async_copy(w_hbm.at[pl.ds(first, F)], w_ref, sem.at[0])
    copy.start()
    out_ref[F : F + 24] = history_ref[...].astype(F32).reshape(24, 128).astype(BF)
    rest = jnp.concatenate([taps_ref[...], jnp.zeros((3, 128), F32)], axis=0)
    for k in range(3):
        piece = rest.astype(BF)
        out_ref[F + 24 + 8 * k : F + 32 + 8 * k] = piece
        rest = rest - piece.astype(F32)
    copy.wait()
    out_ref[:F] = w_ref[...]


def wide_heads(row):
    spot = lanes(1)
    return jnp.concatenate(
        [jnp.where(spot < PS, row[:, 2 * j : 2 * j + 1], row[:, 2 * j + 1 : 2 * j + 2]) for j in range(HEADS // 2)],
        axis=1,
    )


def setup_kernel(where_ref, *refs):
    got = refs[:PEERS]
    conv_ref, bias_ref, rate_ref, skip_ref, norm_ref, history_ref, w_ref, past_ref = refs[PEERS:]
    place = lax.rem(where_ref[1], PEERS)
    for k in range(PEERS):
        mine = got[k][...].astype(F32)
        for i in range(1, PEERS):
            mine = jnp.where(place == i, got[(k - i) % PEERS][...].astype(F32), mine)
        span = slice(k * 128, k * 128 + 128)
        w_ref[:, span] = mine[:F].astype(BF)
        for j in range(3):
            past_ref[3 + j, :, span] = mine[F + R * j : F + R * j + R]
        taps = mine[F + 24 : F + 32] + mine[F + 32 : F + 40] + mine[F + 40 : F + 48]
        past_ref[6, 5:8, span] = taps[:3]
        past_ref[7, 0:2, span] = taps[3:5]
    for j in range(3):
        past_ref[j] = history_ref[j].astype(F32)
    past_ref[6, 0:5] = conv_ref[...]
    past_ref[7, 2:3] = wide_heads(bias_ref[...])
    past_ref[7, 3:4] = wide_heads(rate_ref[...])
    past_ref[7, 4:5] = wide_heads(skip_ref[...])
    past_ref[7, 5:6] = norm_ref[...]
    past_ref[7, 6:8] = jnp.zeros((2, C), F32)


def group_sum(parts_ref, first):
    pairs = []
    for g in range(G):
        pair = parts_ref[first + g * PEERS, -R:, :128].astype(F32)
        for k in range(1, PEERS):
            pair = pair + parts_ref[first + g * PEERS + k, -R:, :128].astype(F32)
        pairs.append(lax.rsqrt((pair[0:1] + pair[1:2]) / (DI // G) + EPS))
    scales = jnp.concatenate(pairs + pairs, axis=0).T
    rows = parts_ref.shape[1] - R
    total = jnp.zeros((rows, 256), F32)
    for g in range(G):
        part = parts_ref[first + g * PEERS, :rows].astype(F32)
        for k in range(1, PEERS):
            part = part + parts_ref[first + g * PEERS + k, :rows].astype(F32)
        total = total + part * scales[:rows, g : g + 1]
    return total


def half_kernel(parts_ref, out_ref):
    out_ref[...] = group_sum(parts_ref, 0).astype(BF)


def next_kernel(step, where_ref, mine_ref, other_ref, hid_ref, *refs):
    even = lax.rem(where_ref[1], 2) == 0
    mine, other = mine_ref[...].astype(F32), other_ref[...].astype(F32)
    mixed = jnp.concatenate([jnp.where(even, mine, other), jnp.where(even, other, mine)], axis=1)
    refs[-1][:, NZ:] = mixed.astype(BF)
    project(fresh_rows(hid_ref, step) + mixed, *refs)


def silu(value):
    return value / (1.0 + jnp.exp(-value))


def across(left, right):
    return lax.dot_general(left, right, (((1,), (1,)), ((), ())), preferred_element_type=F32)


def convolve(past_ref, first, fresh, params, tap):
    total = fresh * params[tap + 3 : tap + 4] + params[tap + 4 : tap + 5]
    for k in range(3):
        total = total + past_ref[first + k] * params[tap + k : tap + k + 1]
    return silu(total)


def read_kernel(
    has_mixed,
    where_ref,
    zx_hbm,
    past_hbm,
    state_hbm,
    out_ref,
    kept_ref,
    change_ref,
    *rest,
):
    zx_ref, past_ref, state_ref, small_sems, row_sems = rest[-5:]
    arrive = pltpu.make_async_copy(zx_hbm, zx_ref, small_sems.at[0])
    small = pltpu.make_async_copy(past_hbm, past_ref, small_sems.at[1])
    arrive.start()
    small.start()
    large = [pltpu.make_async_copy(state_hbm.at[r], state_ref.at[r], row_sems.at[r]) for r in range(R)]
    for copy in large:
        copy.start()
    arrive.wait()
    z = zx_ref[0][:, :NZ].astype(F32)
    for k in range(1, DP):
        z = z + zx_ref[k][:, :NZ].astype(F32)
    tail = z[:, NZ - 128 :]
    squares = tail[:, HEADS : HEADS + 1] + tail[:, HEADS + 1 : HEADS + 2]
    z = z * lax.rsqrt(squares / D + EPS)
    gate = z[:, :C]
    inner = z[:, C : 2 * C]
    bc = z[:, 2 * C : 2 * C + 2 * N]
    small.wait()
    params = past_ref[6:].reshape(2 * R, C)
    conv_x = convolve(past_ref, 0, inner, params, 0)
    conv_bc = convolve(past_ref, 3, bc, params, 5)
    for k in range(2):
        kept_ref[k] = past_ref[k + 1]
        kept_ref[3 + k] = past_ref[4 + k]
    kept_ref[2] = inner
    kept_ref[5] = bc
    kept_ref[6:] = past_ref[6:]
    head = params[10:13]
    gain = params[13:14]
    spot = lanes(R)
    columns = [z[:, NZ - 128 + k : NZ - 127 + k] for k in range(HEADS)]
    raw = jnp.concatenate([jnp.where(spot < PS, *columns[2 * j : 2 * j + 2]) for j in range(HEADS // 2)], axis=1)
    raw = raw + head[0:1]
    step_size = jnp.maximum(raw, 0.0) + jnp.log1p(jnp.exp(-jnp.abs(raw)))
    decay = jnp.exp(-step_size * head[1:2])
    added = step_size * conv_x
    change_ref[0] = decay
    change_ref[1] = added
    change_ref[2] = conv_bc
    b, c = conv_bc[:, :N], conv_bc[:, N:]
    high, low = split_pair(c)
    probe = jnp.concatenate([high, low], axis=0).astype(BF)
    row = lax.broadcasted_iota(jnp.int32, (R, C), 0)
    sums = jnp.zeros((R, C), F32)
    for r in range(R):
        large[r].wait()
        old = state_ref[r]
        high = old.astype(BF)
        low = (old - high.astype(F32)).astype(BF)
        total = across(probe, high) + across(probe, low)
        sums = jnp.where(row == r, total[:R] + total[R:], sums)
    read = decay * sums + added * jnp.sum(b * c, axis=-1, keepdims=True) + head[2:3] * conv_x
    gated = read * silu(gate)
    high, low = split_pair(jnp.sum(gated * gated, axis=-1, keepdims=True))
    message = (gated * gain).astype(BF)
    pair = jnp.where(spot == 0, high, jnp.where(spot == 1, low, 0.0)).astype(BF)
    for k in range(DP):
        out_ref[k, :, :C] = message
        out_ref[k, :, C:] = pair
    if has_mixed:
        mixed_ref = rest[0]
        slot = where_ref[1]
        half = pl.multiple_of(NZ + lax.rem(slot, 2) * 256, 128)
        mixed_ref[...] = zx_ref[slot // 2, :, pl.ds(half, 256)]


def update_kernel(change_ref, state_ref, new_ref, left_ref):
    r = pl.program_id(0)

    @pl.when(r == 0)
    def _():
        high, low = split_pair(change_ref[1])
        left_ref[...] = jnp.concatenate([high, low, high], axis=0).T.astype(BF)

    high, low = split_pair(change_ref[2, :, :N])
    right = jnp.concatenate([high, high, low], axis=0)
    row = lax.rem(lax.broadcasted_iota(jnp.int32, (3 * R, N), 0), R)
    outer = jnp.dot(left_ref[...], jnp.where(row == r, right, 0.0).astype(BF), preferred_element_type=F32)
    decay = change_ref[0, pl.ds(r, 1)]
    for k in range(HEADS):
        span = slice(k * PS, k * PS + PS)
        new_ref[0, span] = decay[:, k * PS : k * PS + 1] * state_ref[0, span] + outer[span]


def out_parts(q_ref, w_ref):
    part = jnp.dot(q_ref[:, :C], w_ref[...], preferred_element_type=F32).astype(BF)
    pair = q_ref[:, C:].astype(F32)
    pair = jnp.concatenate([pair, jnp.zeros_like(pair)], axis=0).T[:R]
    return part, pair


def out_kernel(q_ref, w_ref, out_ref):
    part, pair = out_parts(q_ref, w_ref)
    pair = jnp.concatenate([pair, pair], axis=1).astype(BF)
    for k in range(TP):
        half = (k % 2) * 256
        out_ref[k, :ROWS] = part[:, half : half + 256]
        out_ref[k, ROWS:] = pair


def last_kernel(where_ref, q_ref, w_ref, out_ref):
    part, pair = out_parts(q_ref, w_ref)
    out_ref[...] = jnp.zeros_like(out_ref)
    me = where_ref[0]
    for k in range(DP):
        mine = jnp.concatenate([pair[:, k * R : k * R + R], jnp.zeros((R, 256 - R), F32)], axis=1).astype(BF)
        for half in range(2):
            slot = k * TP + 2 * me + half
            out_ref[slot, :R] = part[k * R : k * R + R, half * 256 : half * 256 + 256]
            out_ref[slot, R:] = mine


def finish_kernel(where_ref, parts_ref, out_ref):
    out_ref[...] = group_sum(parts_ref, (where_ref[1] // 2) * TP).astype(BF)


def struct(shape, dtype):
    return jax.ShapeDtypeStruct(shape, dtype)


def call(kernel, outs, operands, remote=0, compiler_params=PARAMS, **extra):
    near = operands[: len(operands) - remote]
    return pl.pallas_call(
        kernel,
        out_shape=outs,
        in_specs=[SM if o.dtype == jnp.int32 else VM for o in near] + [HB] * remote,
        out_specs=jax.tree.map(lambda _: VM, outs),
        compiler_params=compiler_params,
        **extra,
    )(*operands)


def swap(value, axis):
    return lax.all_to_all(value, axis, 0, 0, tiled=True)


def decode_matrix(codes, exponents, block):
    rows, cols = codes.shape
    blocked = codes.astype(jnp.float32).reshape(rows // block, block, cols // block, block)
    scales = jnp.exp2(exponents.astype(jnp.float32))
    return (blocked * scales[:, None, :, None]).reshape(rows, cols)


def group_slabs(slab):
    needed = [[2 * g, 2 * g + 1, 8 + 2 * g, 9 + 2 * g] for g in range(G)]
    got = []
    for turn in range(PEERS):
        pairs = [(needed[g][(i + turn) % PEERS], g * PEERS + i) for g in range(G) for i in range(PEERS)]
        got.append(lax.ppermute(slab, "tp", pairs))
    return got


def body(
    hidden_in,
    pre_gain,
    w_zx,
    zx_codes,
    zx_exponents,
    w_bc,
    w_dt,
    conv_x,
    conv_bc,
    dt_bias,
    decay_rate,
    skip_gain,
    conv_state_x,
    conv_state_bc,
    ssm_state,
    norm_gain,
    w_out,
    out_codes,
    out_exponents,
):
    replica = lax.axis_index("dp")
    slot = lax.axis_index("tp")
    where = jnp.stack([replica, slot]).astype(jnp.int32)

    packed = call(pack_kernel, struct((TP, 2, F // TP, C), BF), [zx_codes])
    split = jnp.moveaxis(hidden_in.reshape(STEPS, R, DP, F), 2, 0)
    split, w_bc = lax.optimization_barrier((split, w_bc))
    hid = swap(split, "dp")
    slab = pl.pallas_call(
        slab_kernel,
        out_shape=struct((SLAB, 128), BF),
        in_specs=[SM, HB, VM, VM],
        out_specs=VM,
        scratch_shapes=[pltpu.VMEM((F, 128), BF), pltpu.SemaphoreType.DMA((1,))],
        compiler_params=WHOLE,
    )(where, w_bc, conv_bc, jnp.moveaxis(conv_state_bc, 1, 0))
    got = group_slabs(slab)
    packed, hid = lax.optimization_barrier((packed, hid))
    traded = swap(packed, "tp")
    bc_weights, past = call(
        setup_kernel,
        [struct((F, 2 * N), BF), struct((8, R, C), F32)],
        [
            where,
            *got,
            conv_x,
            dt_bias[None],
            decay_rate[None],
            skip_gain[None],
            norm_gain[None],
            jnp.moveaxis(conv_state_x, 1, 0),
        ],
    )

    w_rows = jnp.transpose(lax.dynamic_slice_in_dim(w_zx, replica * F, F, 0), (1, 0, 2))
    scales = jnp.repeat(jnp.exp2(zx_exponents.astype(F32)), BLK, axis=2).reshape(8, C)
    zx_weights = pl.pallas_call(
        decode_kernel,
        out_shape=struct((F, 2 * C), BF),
        grid=(F // BLK,),
        in_specs=[
            pl.BlockSpec((TP * BLK // F, 2, F // TP, C), lambda k: (k, 0, 0, 0)),
            pl.BlockSpec((2, BLK, C), lambda k: (0, k, 0)),
            pl.BlockSpec((8, C), lambda k: (0, 0)),
        ],
        out_specs=pl.BlockSpec((BLK, 2 * C), lambda k: (k, 0)),
        compiler_params=WHOLE,
    )(traded, w_rows, scales)
    dt_weights = jnp.pad(lax.dynamic_slice_in_dim(w_dt, replica * F, F, 0), ((0, 0), (0, 128 - HEADS)))
    w_out_cols = lax.dynamic_slice_in_dim(w_out, replica * 512, 512, 1)
    out_weights = (w_out_cols.astype(F32) + decode_matrix(out_codes, out_exponents, BLK)).astype(BF)

    gain = lax.dynamic_slice_in_dim(pre_gain, replica * F, F, 0)[None]
    state = ssm_state.reshape(R, C, N)
    fixed = [gain, zx_weights, bc_weights, dt_weights]
    results = []
    mine = other = None
    for step in range(STEPS):
        if step == 0:
            zx = call(first_kernel, struct((ROWS, NZ), BF), [hid, *fixed])
        else:
            zx = call(
                functools.partial(next_kernel, step),
                struct((ROWS, NZ + 512), BF),
                [where, mine, other, hid, *fixed],
            )
        zx = swap(zx.reshape(DP, R, -1), "dp")
        outs = [
            struct((DP, R, NQ), BF),
            struct(past.shape, F32),
            struct((3, R, C), F32),
        ]
        if step > 0:
            outs.append(struct((R, 256), BF))
        q, past, change, *mixed = call(
            functools.partial(read_kernel, step > 0),
            outs,
            [where, zx, past, state],
            remote=3,
            compiler_params=WHOLE,
            scratch_shapes=[
                pltpu.VMEM(zx.shape, BF),
                pltpu.VMEM(past.shape, F32),
                pltpu.VMEM(state.shape, F32),
                pltpu.SemaphoreType.DMA((2,)),
                pltpu.SemaphoreType.DMA((R,)),
            ],
        )
        results += mixed
        block = pl.BlockSpec((1, C, N), lambda r: (r, 0, 0))
        state = pl.pallas_call(
            update_kernel,
            out_shape=struct(state.shape, F32),
            grid=(R,),
            in_specs=[pl.BlockSpec((3, R, C), lambda r: (0, 0, 0)), block],
            out_specs=block,
            scratch_shapes=[pltpu.VMEM((C, 3 * R), BF)],
            compiler_params=WHOLE,
            cost_estimate=pl.CostEstimate(flops=4 * 10**9, transcendentals=0, bytes_accessed=8 * 2**20),
        )(change, state)
        q = swap(q, "dp").reshape(ROWS, NQ)
        if step + 1 < STEPS:
            parts = swap(call(out_kernel, struct((TP, ROWS + R, 256), BF), [q, out_weights]), "tp")
            mine = call(half_kernel, struct((ROWS, 256), BF), [parts])
            other = lax.ppermute(mine, "tp", [(k, k ^ 1) for k in range(TP)])
        else:
            tiles = call(last_kernel, struct((DP * TP, 2 * R, 256), BF), [where, q, out_weights])
            tiles = lax.all_to_all(tiles, ("dp", "tp"), 0, 0, tiled=True)
            results.append(call(finish_kernel, struct((R, 256), BF), [where, tiles]))
    return (jnp.stack(results), state.reshape(ssm_state.shape))


def solution(mesh):
    return jax.shard_map(
        body,
        mesh=mesh,
        in_specs=(
            P(None, "dp", None),
            P(),
            P(None, None, "tp"),
            P(("dp", "tp"), None, None),
            P("dp", None, "tp"),
            P(None, "tp"),
            P(None, "tp"),
            P(None, "tp"),
            P(None, "tp"),
            P("tp"),
            P("tp"),
            P("tp"),
            P("dp", None, "tp"),
            P("dp", None, "tp"),
            P("dp", "tp", None, None),
            P("tp"),
            P("tp", None),
            P("tp", "dp"),
            P("tp", "dp"),
        ),
        out_specs=(P(None, "dp", "tp"), P("dp", "tp", None, None)),
        check_vma=False,
    )
```

time: 319 us -> 262 us (0.82)
  blocking collectives: 155 us -> 86.9 us
  local copies, waits for them, and re-layouts: 43.4 us -> 12.7 us
  Pallas kernels: 45.3 us -> 70.6 us
  waiting for transfers between devices: 26.8 us -> 41.8 us
  starting transfers between devices: 31 us -> 44.6 us
  other arithmetic: 15.4 us -> 2.59 us
    all_to_all x9 -> x6, blocking collectives: 132 us -> 86.9 us  [swap(): return lax.all_to_all(value, axis, 0, 0, tiled=True)]
    pallas_call x0 -> x6, Pallas kernels: none -> 35.6 us  [the longest x4 29.5 us: body(): pl.pallas_call(update_kernel, out_shape=struct(state.shape, F32), grid=(R...]
    all_to_all x1 -> x0, blocking collectives: 22.7 us -> none  [body(): tiles = lax.all_to_all(tiles, ('dp', 'tp'), 0, 0, tiled=True)]
    unnamed x39 -> x55, local copies, waits for them, and re-layouts: 25.7 us -> 7.92 us
    all_to_all x3 -> x7, starting transfers between devices: 17.3 us -> 32.5 us  [swap(): return lax.all_to_all(value, axis, 0, 0, tiled=True)]
    convert_element_type x6 -> x0, other arithmetic: 13.1 us -> none  [the longest x1 8.94 us: decode_pairs(): codes.astype(jnp.float32)]
    convert_element_type x1 -> x0, local copies, waits for them, and re-layouts: 10.3 us -> none  [decode_pairs(): codes.astype(jnp.float32)]
    pallas_call x13 -> x18, Pallas kernels: 45.3 us -> 35 us  [call(): pl.pallas_call(kernel, out_shape=outs, in_specs=[SM if o.dtype == jnp.int...]
  transfers between devices with their start and end apart: 8 -> 15, of which waited for: 3 -> 13; matrix products, arithmetic and copies ran while one was open for 8% -> 3% of each run, Pallas kernels for 0% -> 13%
where the time goes in v2:
time: 262 us; the launch traced here: 260 us
  blocking collectives  86.9 us (33%)
  Pallas kernels  70.6 us (27%)
  starting transfers between devices  44.6 us (17%)
  waiting for transfers between devices  41.8 us (16%)
  local copies, waits for them, and re-layouts  12.7 us (5%)
    all_to_all x6, blocking collectives, swap(): return lax.all_to_all(value, axis, 0, 0, tiled=True)  86.9 us
    pallas_call x18, Pallas kernels, call(): pl.pallas_call(kernel, out_shape=outs, in_specs=[SM if o.dtype == jnp.int...  35 us
    all_to_all x7, starting transfers between devices, swap(): return lax.all_to_all(value, axis, 0, 0, tiled=True)  32.5 us
    pallas_call x4, Pallas kernels, body(): pl.pallas_call(update_kernel, out_shape=struct(state.shape, F32), grid=(R...  29.5 us
    all_to_all x7, waiting for transfers between devices, swap(): return lax.all_to_all(value, axis, 0, 0, tiled=True)  20.4 us
    all_to_all x1, waiting for transfers between devices, body(): tiles = lax.all_to_all(tiles, ('dp', 'tp'), 0, 0, tiled=True)  11.8 us
    unnamed x55, local copies, waits for them, and re-layouts  7.92 us
    ppermute x4, waiting for transfers between devices, group_slabs(): got.append(lax.ppermute(slab, 'tp', pairs))  7.05 us
  transfers between devices with their start and end apart: 15, of which 13 were waited for; matrix products, arithmetic and copies ran while one was open for 3% of the time, Pallas kernels for 13%

profile of v2, /device:TPU:1, one launch (start us, length us, event | category | flops | bytes accessed | tf_op | source)
XLA Modules:
  0.0 260.1 jit_solution(15237848512178626821)
XLA Ops:
  2.4 8.2 %all-to-all-start = ((bf16[8,4,8,512]{3,2,1,0:T(8,128)(2,1)}), bf16[8,4,8,512]{3,2,1,0:T(8,128)(2,1)S(1)}, u32[]{:S(2)}, u32[]{:S(2)}) async-start(bf16[8,4,8,512]{3,2,1,0:T(8,128)(2,1)} %bitcast.44), calls=%async_computation | async-start | bytes 524288 | tf_op jit(solution)/shard_map/all_to_all | solution.py:324
  13.0 4.9 %all-to-all-done.hid_ref = bf16[8,4,8,512]{3,2,1,0:T(8,128)(2,1)S(1)} async-done(((bf16[8,4,8,512]{3,2,1,0:T(8,128)(2,1)}), bf16[8,4,8,512]{3,2,1,0:T(8,128)(2,1)S(1)}, u32[]{:S(2)}, u32[]{:S(2)}) %all-to-all-start) | async-done | bytes 262176 | tf_op jit(solution)/shard_map/all_to_all | solution.py:324
  18.0 7.2 %all-to-all-start.1 = ((bf16[16,2,32,512]{3,2,1,0:T(8,128)(2,1)}), bf16[16,2,32,512]{3,2,1,0:T(8,128)(2,1)}, u32[]{:S(2)}, u32[]{:S(2)}) async-start(bf16[16,2,32,512]{3,2,1,0:T(8,128)(2,1)} %shard_map.194), calls=%async_computation.1 | async-start | bytes 2097152 | tf_op jit(solution)/shard_map/all_to_all | solution.py:324
  25.8 2.3 shard_map.196
  29.8 1.8 collective-permute-start.2
  34.8 2.0 constant_dynamic-slice_fusion.1
  38.0 2.6 %collective-permute-done.3.refs_3_ = bf16[560,128]{1,0:T(8,128)(2,1)S(1)} collective-permute-done((bf16[560,128]{1,0:T(8,128)(2,1)}, bf16[560,128]{1,0:T(8,128)(2,1)S(1)}, u32[]{:S(2)}, u32[]{:S(2)}) %collective-permute-start.3) | collective-permute-done | bytes 143392 | tf_op jit(solution)/shard_map/ppermute | solution.py:339
  40.6 3.8 %collective-permute-done.2.refs_2_ = bf16[560,128]{1,0:T(8,128)(2,1)S(1)} collective-permute-done((bf16[560,128]{1,0:T(8,128)(2,1)}, bf16[560,128]{1,0:T(8,128)(2,1)S(1)}, u32[]{:S(2)}, u32[]{:S(2)}) %collective-permute-start.2) | collective-permute-done | bytes 143392 | tf_op jit(solution)/shard_map/ppermute | solution.py:339
  46.7 3.7 %shard_map.195.refs_1_ = bf16[512,1024]{1,0:T(8,128)(2,1)} custom-call(bf16[16,2,32,512]{3,2,1,0:T(8,128)(2,1)} %all-to-all-done.1.codes_ref, bf16[2,512,512]{2,1,0:T(8,128)(2,1)} %bitcast.60, f32[8,512]{1,0:T(8,128)} %bitcast.65), custom_call_target="tpu_custom_call" | custom-call | tf_op jit(solution)/shard_map/pallas_call | solution.py:400
  52.8 3.4 %all-to-all-start.2 = ((bf16[8,8,1664]{2,1,0:T(8,128)(2,1)}), bf16[8,8,1664]{2,1,0:T(8,128)(2,1)S(1)}, u32[]{:S(2)}, u32[]{:S(2)}) async-start(bf16[8,8,1664]{2,1,0:T(8,128)(2,1)} %bitcast.11), calls=%async_computation.2 | async-start | bytes 425984 | tf_op jit(solution)/shard_map/all_to_all | solution.py:324
  56.2 7.7 %all-to-all-done.2.zx_hbm = bf16[8,8,1664]{2,1,0:T(8,128)(2,1)S(1)} async-done(((bf16[8,8,1664]{2,1,0:T(8,128)(2,1)}), bf16[8,8,1664]{2,1,0:T(8,128)(2,1)S(1)}, u32[]{:S(2)}, u32[]{:S(2)}) %all-to-all-start.2) | async-done | bytes 213024 | tf_op jit(solution)/shard_map/all_to_all | solution.py:324
  64.6 5.7 %shard_map.199 = (bf16[8,8,640]{2,1,0:T(8,128)(2,1)}, f32[8,8,512]{2,1,0:T(8,128)}, f32[3,8,512]{2,1,0:T(8,128)}) custom-call(s32[2]{0:T(128)} %pad_add_fusion.where_ref, bf16[8,8,1664]{2,1,0:T(8,128)(2,1)} %copy-done.19, f32[8,8,512]{2,1,0:T(8,128)} %copy-done.4, f32[8,512,256]{2,1,0:T(8,128)} %bitcast.61), custom_call_target="tpu_custom_call" | custom-call | tf_op jit(solution)/shard_map/pallas_call | solution.py:313
  70.3 3.5 %all-to-all-start.3 = ((bf16[8,8,640]{2,1,0:T(8,128)(2,1)}), bf16[8,8,640]{2,1,0:T(8,128)(2,1)S(1)}, u32[]{:S(2)}, u32[]{:S(2)}) async-start(bf16[8,8,640]{2,1,0:T(8,128)(2,1)} %get-tuple-element.28), calls=%async_computation.3 | async-start | bytes 163840 | tf_op jit(solution)/shard_map/all_to_all | solution.py:324
  75.4 5.0 %all-to-all-done.3 = bf16[8,8,640]{2,1,0:T(8,128)(2,1)S(1)} async-done(((bf16[8,8,640]{2,1,0:T(8,128)(2,1)}), bf16[8,8,640]{2,1,0:T(8,128)(2,1)S(1)}, u32[]{:S(2)}, u32[]{:S(2)}) %all-to-all-start.3) | async-done | bytes 81952 | tf_op jit(solution)/shard_map/all_to_all | solution.py:324
  80.6 18.5 %all_to_all.70.parts_ref = bf16[16,72,256]{2,1,0:T(8,128)(2,1)S(1)} all-to-all(bf16[16,72,256]{2,1,0:T(8,128)(2,1)S(1)} %shard_map.200), channel_id=1, replica_groups=mesh['dp'=8,'tp'=16] {'tp'}, dimensions={0} | all-to-all | bytes 1179648 | tf_op jit(solution)/shard_map/all_to_all | solution.py:324
  102.3 3.4 %all-to-all-start.5 = ((bf16[8,8,2176]{2,1,0:T(8,128)(2,1)}), bf16[8,8,2176]{2,1,0:T(8,128)(2,1)S(1)}, u32[]{:S(2)}, u32[]{:S(2)}) async-start(bf16[8,8,2176]{2,1,0:T(8,128)(2,1)} %bitcast.14), calls=%async_computation.5 | async-start | bytes 557056 | tf_op jit(solution)/shard_map/all_to_all | solution.py:324
  105.8 7.4 %shard_map.203.state_hbm.state_ref = f32[8,512,256]{2,1,0:T(8,128)} custom-call(f32[3,8,512]{2,1,0:T(8,128)} %get-tuple-element.30.change_ref, f32[8,512,256]{2,1,0:T(8,128)} %bitcast.62), custom_call_target="tpu_custom_call" | custom-call | flops 4000000000 | bytes 8388608 | tf_op jit(solution)/shard_map/pallas_call | solution.py:454
  114.8 5.7 %shard_map.204 = (bf16[8,8,640]{2,1,0:T(8,128)(2,1)}, f32[8,8,512]{2,1,0:T(8,128)}, f32[3,8,512]{2,1,0:T(8,128)}, bf16[8,256]{1,0:T(8,128)(2,1)}) custom-call(s32[2]{0:T(128)} %pad_add_fusion.where_ref, bf16[8,8,2176]{2,1,0:T(8,128)(2,1)} %copy-done.16, f32[8,8,512]{2,1,0:T(8,128)} %get-tuple-element.29.past_hbm, f32[8,512,256]{2,1,0:T(8,128)} %shard_map.203.state_hbm.state_ref), custom_call_target="tpu_custom_call" | custom-call | tf_op jit(solution)/shard_map/pallas_call | solution.py:313
  120.5 12.2 %all_to_all.71 = bf16[8,8,640]{2,1,0:T(8,128)(2,1)S(1)} all-to-all(bf16[8,8,640]{2,1,0:T(8,128)(2,1)} %get-tuple-element.32), channel_id=1, replica_groups=mesh['dp'=8,'tp'=16] {'dp'}, dimensions={0} | all-to-all | bytes 163840 | tf_op jit(solution)/shard_map/all_to_all | solution.py:324
  133.0 15.8 %all_to_all.72.parts_ref = bf16[16,72,256]{2,1,0:T(8,128)(2,1)S(1)} all-to-all(bf16[16,72,256]{2,1,0:T(8,128)(2,1)S(1)} %shard_map.205), channel_id=1, replica_groups=mesh['dp'=8,'tp'=16] {'tp'}, dimensions={0} | all-to-all | bytes 1179648 | tf_op jit(solution)/shard_map/all_to_all | solution.py:324
  152.0 3.4 %all-to-all-start.8 = ((bf16[8,8,2176]{2,1,0:T(8,128)(2,1)}), bf16[8,8,2176]{2,1,0:T(8,128)(2,1)S(1)}, u32[]{:S(2)}, u32[]{:S(2)}) async-start(bf16[8,8,2176]{2,1,0:T(8,128)(2,1)} %bitcast.17), calls=%async_computation.8 | async-start | bytes 557056 | tf_op jit(solution)/shard_map/all_to_all | solution.py:324
  155.4 7.4 %shard_map.208.state_hbm.state_ref = f32[8,512,256]{2,1,0:T(8,128)} custom-call(f32[3,8,512]{2,1,0:T(8,128)} %get-tuple-element.34.change_ref, f32[8,512,256]{2,1,0:T(8,128)} %shard_map.203.state_hbm.state_ref), custom_call_target="tpu_custom_call" | custom-call | flops 4000000000 | bytes 8388608 | tf_op jit(solution)/shard_map/pallas_call | solution.py:454
  164.4 5.7 %shard_map.209 = (bf16[8,8,640]{2,1,0:T(8,128)(2,1)}, f32[8,8,512]{2,1,0:T(8,128)}, f32[3,8,512]{2,1,0:T(8,128)}, bf16[8,256]{1,0:T(8,128)(2,1)}) custom-call(s32[2]{0:T(128)} %pad_add_fusion.where_ref, bf16[8,8,2176]{2,1,0:T(8,128)(2,1)} %copy-done.17, f32[8,8,512]{2,1,0:T(8,128)} %get-tuple-element.33.past_hbm, f32[8,512,256]{2,1,0:T(8,128)} %shard_map.208.state_hbm.state_ref), custom_call_target="tpu_custom_call" | custom-call | tf_op jit(solution)/shard_map/pallas_call | solution.py:313
  170.2 12.3 %all_to_all.73 = bf16[8,8,640]{2,1,0:T(8,128)(2,1)S(1)} all-to-all(bf16[8,8,640]{2,1,0:T(8,128)(2,1)} %get-tuple-element.36), channel_id=1, replica_groups=mesh['dp'=8,'tp'=16] {'dp'}, dimensions={0} | all-to-all | bytes 163840 | tf_op jit(solution)/shard_map/all_to_all | solution.py:324
  182.8 15.7 %all_to_all.74.parts_ref = bf16[16,72,256]{2,1,0:T(8,128)(2,1)S(1)} all-to-all(bf16[16,72,256]{2,1,0:T(8,128)(2,1)S(1)} %shard_map.210), channel_id=1, replica_groups=mesh['dp'=8,'tp'=16] {'tp'}, dimensions={0} | all-to-all | bytes 1179648 | tf_op jit(solution)/shard_map/all_to_all | solution.py:324
  201.9 3.4 %all-to-all-start.11 = ((bf16[8,8,2176]{2,1,0:T(8,128)(2,1)}), bf16[8,8,2176]{2,1,0:T(8,128)(2,1)S(1)}, u32[]{:S(2)}, u32[]{:S(2)}) async-start(bf16[8,8,2176]{2,1,0:T(8,128)(2,1)} %bitcast.20), calls=%async_computation.11 | async-start | bytes 557056 | tf_op jit(solution)/shard_map/all_to_all | solution.py:324
  205.4 7.4 %shard_map.213.state_hbm.state_ref = f32[8,512,256]{2,1,0:T(8,128)} custom-call(f32[3,8,512]{2,1,0:T(8,128)} %get-tuple-element.38.change_ref, f32[8,512,256]{2,1,0:T(8,128)} %shard_map.208.state_hbm.state_ref), custom_call_target="tpu_custom_call" | custom-call | flops 4000000000 | bytes 8388608 | tf_op jit(solution)/shard_map/pallas_call | solution.py:454
  214.4 5.7 %shard_map.214 = (bf16[8,8,640]{2,1,0:T(8,128)(2,1)}, f32[8,8,512]{2,1,0:T(8,128)}, f32[3,8,512]{2,1,0:T(8,128)}, bf16[8,256]{1,0:T(8,128)(2,1)}) custom-call(s32[2]{0:T(128)} %pad_add_fusion.where_ref, bf16[8,8,2176]{2,1,0:T(8,128)(2,1)} %copy-done.18, f32[8,8,512]{2,1,0:T(8,128)} %get-tuple-element.37.past_hbm, f32[8,512,256]{2,1,0:T(8,128)} %shard_map.213.state_hbm.state_ref), custom_call_target="tpu_custom_call" | custom-call | tf_op jit(solution)/shard_map/pallas_call | solution.py:313
  220.1 12.3 %all_to_all.75 = bf16[8,8,640]{2,1,0:T(8,128)(2,1)S(1)} all-to-all(bf16[8,8,640]{2,1,0:T(8,128)(2,1)} %get-tuple-element.40), channel_id=1, replica_groups=mesh['dp'=8,'tp'=16] {'dp'}, dimensions={0} | all-to-all | bytes 163840 | tf_op jit(solution)/shard_map/all_to_all | solution.py:324
  234.2 5.5 %all-to-all-start.13 = ((bf16[128,16,256]{2,1,0:T(8,128)(2,1)}), bf16[128,16,256]{2,1,0:T(8,128)(2,1)S(1)}, u32[]{:S(2)}, u32[]{:S(2)}) async-start(bf16[128,16,256]{2,1,0:T(8,128)(2,1)} %shard_map.215), calls=%async_computation.13 | async-start | bytes 2097152 | tf_op jit(solution)/shard_map/all_to_all | solution.py:471
  239.7 7.4 %shard_map.217 = f32[8,512,256]{2,1,0:T(8,128)} custom-call(f32[3,8,512]{2,1,0:T(8,128)} %get-tuple-element.41.change_ref, f32[8,512,256]{2,1,0:T(8,128)} %shard_map.213.state_hbm.state_ref), custom_call_target="tpu_custom_call" | custom-call | flops 4000000000 | bytes 8388608 | tf_op jit(solution)/shard_map/pallas_call | solution.py:454
  247.0 11.8 %all-to-all-done.13.parts_ref = bf16[128,16,256]{2,1,0:T(8,128)(2,1)S(1)} async-done(((bf16[128,16,256]{2,1,0:T(8,128)(2,1)}), bf16[128,16,256]{2,1,0:T(8,128)(2,1)S(1)}, u32[]{:S(2)}, u32[]{:S(2)}) %all-to-all-start.13) | async-done | bytes 1048608 | tf_op jit(solution)/shard_map/all_to_all | solution.py:471
  (95 shorter events, 36.2 us)
Async XLA Ops:
  0.6 32.5 %copy-start = (bf16[4096,8]{0,1:T(8,128)(2,1)S(1)}, bf16[4096,8]{0,1:T(8,128)(2,1)}, u32[]{:S(2)}) copy-start(bf16[4096,8]{0,1:T(8,128)(2,1)} %param.25) | copy-start | bytes 196612
  0.6 32.5 %copy-start.21 = (s32[4,2,4]{2,1,0:T(2,128)S(1)}, s32[4,2,4]{2,1,0:T(2,128)}, u32[]{:S(2)}) copy-start(s32[4,2,4]{2,1,0:T(2,128)} %param.23) | copy-start | bytes 388
  2.4 15.6 %all-to-all-start = ((bf16[8,4,8,512]{3,2,1,0:T(8,128)(2,1)}), bf16[8,4,8,512]{3,2,1,0:T(8,128)(2,1)S(1)}, u32[]{:S(2)}, u32[]{:S(2)}) async-start(bf16[8,4,8,512]{3,2,1,0:T(8,128)(2,1)} %bitcast.44), calls=%async_computation | async-start | bytes 524288 | tf_op jit(solution)/shard_map/all_to_all | solution.py:324
  13.0 32.0 %copy-start.10 = (bf16[8,3,512]{2,0,1:T(8,128)(2,1)S(1)}, bf16[8,3,512]{2,0,1:T(8,128)(2,1)}, u32[]{:S(2)}) copy-start(bf16[8,3,512]{2,0,1:T(8,128)(2,1)} %param.31) | copy-start | bytes 73732
  13.0 32.0 %copy-start.11 = (f32[5,512]{1,0:T(8,128)S(1)}, f32[5,512]{1,0:T(8,128)}, u32[]{:S(2)}) copy-start(f32[5,512]{1,0:T(8,128)} %refs_4_.1) | copy-start | bytes 30724
  13.0 32.0 %copy-start.12 = (f32[512]{0:T(512)S(1)}, f32[512]{0:T(512)}, u32[]{:S(2)}) copy-start(f32[512]{0:T(512)} %param.34) | copy-start | bytes 6148
  13.0 32.0 %copy-start.13 = (f32[8]{0:T(128)S(1)}, f32[8]{0:T(128)}, u32[]{:S(2)}) copy-start(f32[8]{0:T(128)} %param.28) | copy-start | bytes 100
  13.0 32.0 %copy-start.14 = (f32[8]{0:T(128)S(1)}, f32[8]{0:T(128)}, u32[]{:S(2)}) copy-start(f32[8]{0:T(128)} %param.29) | copy-start | bytes 100
  13.0 32.0 %copy-start.15 = (f32[8]{0:T(128)S(1)}, f32[8]{0:T(128)}, u32[]{:S(2)}) copy-start(f32[8]{0:T(128)} %param.30) | copy-start | bytes 100
  18.0 28.8 %all-to-all-start.1 = ((bf16[16,2,32,512]{3,2,1,0:T(8,128)(2,1)}), bf16[16,2,32,512]{3,2,1,0:T(8,128)(2,1)}, u32[]{:S(2)}, u32[]{:S(2)}) async-start(bf16[16,2,32,512]{3,2,1,0:T(8,128)(2,1)} %shard_map.194), calls=%async_computation.1 | async-start | bytes 2097152 | tf_op jit(solution)/shard_map/all_to_all | solution.py:324
  28.1 12.5 %collective-permute-start.3 = (bf16[560,128]{1,0:T(8,128)(2,1)}, bf16[560,128]{1,0:T(8,128)(2,1)S(1)}, u32[]{:S(2)}, u32[]{:S(2)}) collective-permute-start(bf16[560,128]{1,0:T(8,128)(2,1)} %shard_map.196), channel_id=1, source_target_pairs={{9,0},{0,1},{1,2},{8,3},{11,4},{2,5},{3,6},{10,7},{13,8},{4,9},{5,... | collective-permute-start | bytes 430088 | tf_op jit(solution)/shard_map/ppermute | solution.py:339
  29.8 14.6 %collective-permute-start.2 = (bf16[560,128]{1,0:T(8,128)(2,1)}, bf16[560,128]{1,0:T(8,128)(2,1)S(1)}, u32[]{:S(2)}, u32[]{:S(2)}) collective-permute-start(bf16[560,128]{1,0:T(8,128)(2,1)} %shard_map.196), channel_id=1, source_target_pairs={{8,0},{9,1},{0,2},{1,3},{10,4},{11,5},{2,6},{3,7},{12,8},{13,9},{4... | collective-permute-start | bytes 430088 | tf_op jit(solution)/shard_map/ppermute | solution.py:339
  31.6 13.4 %collective-permute-start.1 = (bf16[560,128]{1,0:T(8,128)(2,1)}, bf16[560,128]{1,0:T(8,128)(2,1)S(1)}, u32[]{:S(2)}, u32[]{:S(2)}) collective-permute-start(bf16[560,128]{1,0:T(8,128)(2,1)} %shard_map.196), channel_id=1, source_target_pairs={{1,0},{8,1},{9,2},{0,3},{3,4},{10,5},{11,6},{2,7},{5,8},{12,9},{13... | collective-permute-start | bytes 430088 | tf_op jit(solution)/shard_map/ppermute | solution.py:339
  31.6 13.4 %collective-permute-start = (bf16[560,128]{1,0:T(8,128)(2,1)}, bf16[560,128]{1,0:T(8,128)(2,1)S(1)}, u32[]{:S(2)}, u32[]{:S(2)}) collective-permute-start(bf16[560,128]{1,0:T(8,128)(2,1)} %shard_map.196), channel_id=1, source_target_pairs={{0,0},{1,1},{8,2},{9,3},{2,4},{3,5},{10,6},{11,7},{4,8},{5,9},{12,... | collective-permute-start | bytes 430088 | tf_op jit(solution)/shard_map/ppermute | solution.py:339
  46.7 27.3 %copy-start.20 = (bf16[512,512]{1,0:T(8,128)(2,1)S(1)}, bf16[512,512]{1,0:T(8,128)(2,1)}, u32[]{:S(2)}) copy-start(bf16[512,512]{1,0:T(8,128)(2,1)} %param.36) | copy-start | bytes 1572868
  52.8 11.1 %all-to-all-start.2 = ((bf16[8,8,1664]{2,1,0:T(8,128)(2,1)}), bf16[8,8,1664]{2,1,0:T(8,128)(2,1)S(1)}, u32[]{:S(2)}, u32[]{:S(2)}) async-start(bf16[8,8,1664]{2,1,0:T(8,128)(2,1)} %bitcast.11), calls=%async_computation.2 | async-start | bytes 425984 | tf_op jit(solution)/shard_map/all_to_all | solution.py:324
  70.3 30.3 %copy-start.2 = (bf16[512,1024]{1,0:T(8,128)(2,1)S(1)}, bf16[512,1024]{1,0:T(8,128)(2,1)}, u32[]{:S(2)}) copy-start(bf16[512,1024]{1,0:T(8,128)(2,1)} %shard_map.195.refs_1_) | copy-start | bytes 3145732
  70.3 30.3 %copy-start.6 = (s32[2]{0:T(128)S(1)}, s32[2]{0:T(128)}, u32[]{:S(2)}) copy-start(s32[2]{0:T(128)} %pad_add_fusion.where_ref) | copy-start | bytes 28
  70.3 10.1 %all-to-all-start.3 = ((bf16[8,8,640]{2,1,0:T(8,128)(2,1)}), bf16[8,8,640]{2,1,0:T(8,128)(2,1)S(1)}, u32[]{:S(2)}, u32[]{:S(2)}) async-start(bf16[8,8,640]{2,1,0:T(8,128)(2,1)} %get-tuple-element.28), calls=%async_computation.3 | async-start | bytes 163840 | tf_op jit(solution)/shard_map/all_to_all | solution.py:324
  99.3 1.3 collective-permute-start.4
  102.3 11.7 %all-to-all-start.5 = ((bf16[8,8,2176]{2,1,0:T(8,128)(2,1)}), bf16[8,8,2176]{2,1,0:T(8,128)(2,1)S(1)}, u32[]{:S(2)}, u32[]{:S(2)}) async-start(bf16[8,8,2176]{2,1,0:T(8,128)(2,1)} %bitcast.14), calls=%async_computation.5 | async-start | bytes 557056 | tf_op jit(solution)/shard_map/all_to_all | solution.py:324
  113.1 37.2 %copy-start.7 = (s32[2]{0:T(128)S(1)}, s32[2]{0:T(128)}, u32[]{:S(2)}) copy-start(s32[2]{0:T(128)} %pad_add_fusion.where_ref) | copy-start | bytes 28
  149.0 1.3 collective-permute-start.5
  152.0 11.7 %all-to-all-start.8 = ((bf16[8,8,2176]{2,1,0:T(8,128)(2,1)}), bf16[8,8,2176]{2,1,0:T(8,128)(2,1)S(1)}, u32[]{:S(2)}, u32[]{:S(2)}) async-start(bf16[8,8,2176]{2,1,0:T(8,128)(2,1)} %bitcast.17), calls=%async_computation.8 | async-start | bytes 557056 | tf_op jit(solution)/shard_map/all_to_all | solution.py:324
  162.9 37.4 %copy-start.8 = (s32[2]{0:T(128)S(1)}, s32[2]{0:T(128)}, u32[]{:S(2)}) copy-start(s32[2]{0:T(128)} %pad_add_fusion.where_ref) | copy-start | bytes 28
  198.7 1.5 collective-permute-start.6
  201.9 11.7 %all-to-all-start.11 = ((bf16[8,8,2176]{2,1,0:T(8,128)(2,1)}), bf16[8,8,2176]{2,1,0:T(8,128)(2,1)S(1)}, u32[]{:S(2)}, u32[]{:S(2)}) async-start(bf16[8,8,2176]{2,1,0:T(8,128)(2,1)} %bitcast.20), calls=%async_computation.11 | async-start | bytes 557056 | tf_op jit(solution)/shard_map/all_to_all | solution.py:324
  212.7 19.7 %copy-start.9 = (s32[2]{0:T(128)S(1)}, s32[2]{0:T(128)}, u32[]{:S(2)}) copy-start(s32[2]{0:T(128)} %pad_add_fusion.where_ref) | copy-start | bytes 28
  234.2 24.6 %all-to-all-start.13 = ((bf16[128,16,256]{2,1,0:T(8,128)(2,1)}), bf16[128,16,256]{2,1,0:T(8,128)(2,1)S(1)}, u32[]{:S(2)}, u32[]{:S(2)}) async-start(bf16[128,16,256]{2,1,0:T(8,128)(2,1)} %shard_map.215), calls=%async_computation.13 | async-start | bytes 2097152 | tf_op jit(solution)/shard_map/all_to_all | solution.py:471
  239.6 19.9 %copy-start.22 = (bf16[8,256]{1,0:T(8,128)(2,1)S(1)}, bf16[8,256]{1,0:T(8,128)(2,1)}, u32[]{:S(2)}) copy-start(bf16[8,256]{1,0:T(8,128)(2,1)} %get-tuple-element.31) | copy-start | bytes 12292
  239.7 19.9 %copy-start.23 = (bf16[8,256]{1,0:T(8,128)(2,1)S(1)}, bf16[8,256]{1,0:T(8,128)(2,1)}, u32[]{:S(2)}) copy-start(bf16[8,256]{1,0:T(8,128)(2,1)} %get-tuple-element.35) | copy-start | bytes 12292
  239.7 19.9 %copy-start.24 = (bf16[8,256]{1,0:T(8,128)(2,1)S(1)}, bf16[8,256]{1,0:T(8,128)(2,1)}, u32[]{:S(2)}) copy-start(bf16[8,256]{1,0:T(8,128)(2,1)} %get-tuple-element.39) | copy-start | bytes 12292
  (9 other events, 44.6 us)
